TPU v7x, 32 devices: a whole 2x2x4 slice. The times are simulated.
32 devices in a mesh: band: 4 (over z), space: 8 (over y, x, core).
Axes of the slice: x: 2, y: 2, z: 4, core: 2. Of those that a mesh axis runs over, the one named last changes fastest.
Arguments:
- orbitals: float32 [2, 16, 96, 9216], P(None, 'band', 'space'), may hold values from -6 to 6
- potential: float32 [96, 9216], P('space'), may hold values from -2 to 4
- occupations: float32 [16], P('band'), may hold values from 0.5 to 2
Outputs:
- propagated: float32 [2, 16, 96, 9216], P(None, 'band', 'space')
- density: float32 [96, 9216], P('space')
- hartree: float32 [96, 9216], P('space')
All inputs are finite; a program needn't handle non-finite values.
Results may differ from a plain program's by a relative error of at most 0.0029.
Values may be sent and summed in bfloat16 or wider, within the bound.
No kernel may reach another device: no remote copies, remote signals or barrier semaphores. Data moves between devices by JAX's collectives and lax.ppermute only.
A program may use at most 64 MiB of HBM per device.

v0:
```python
import math

import jax
import jax.numpy as jnp
import numpy as np
from jax import lax
from jax.experimental import pallas as pl
from jax.experimental.pallas import tpu as pltpu
from jax.sharding import PartitionSpec as P

NX = 96
NY = 96
NZ = 96


stencil_coeffs = (-205.0 / 72.0, 8.0 / 5.0, -1.0 / 5.0, 8.0 / 315.0, -1.0 / 560.0)
energy_shift = 6.0
energy_scale = 8.0
bessel_terms = (0.7651976865579666, 0.44005058574493355, 0.11490348493190049)


def from_behind(x, axis, by):
    count = lax.axis_size(axis)
    pairs = [(i, i + by) for i in range(count) if 0 <= i + by < count]
    return lax.ppermute(x, axis, pairs)


def plane_laplace(center, wider):
    reach_cells = len(stencil_coeffs) - 1
    planes = center.shape[-2]
    cells = center.shape[-1]
    spread = wider.astype(jnp.float32)
    middle = spread[..., reach_cells : reach_cells + planes, :]
    summed = 3.0 * stencil_coeffs[0] * center
    for offset in range(1, reach_cells + 1):
        after = spread[..., reach_cells + offset : reach_cells + offset + planes, :]
        before = spread[..., reach_cells - offset : reach_cells - offset + planes, :]
        summed = summed + stencil_coeffs[offset] * (after + before)
    margin = reach_cells * NZ
    padded = jnp.pad(middle, [(0, 0)] * (middle.ndim - 1) + [(margin, margin)])
    z_index = lax.iota(jnp.int32, cells) % NZ
    for offset in range(1, reach_cells + 1):
        stride = offset * NZ
        beyond = padded[..., margin + stride : margin + stride + cells]
        behind = padded[..., margin - stride : margin - stride + cells]
        summed = summed + stencil_coeffs[offset] * (beyond + behind)
        beyond = jnp.where(
            z_index + offset < NZ, padded[..., margin + offset : margin + offset + cells], 0.0
        )
        behind = jnp.where(
            z_index - offset >= 0, padded[..., margin - offset : margin - offset + cells], 0.0
        )
        summed = summed + stencil_coeffs[offset] * (beyond + behind)
    return summed


def scaled_hamiltonian(center, wider, field_values):
    energy = -0.5 * plane_laplace(center, wider) + field_values * center
    return (energy - energy_shift * center) / energy_scale


def slab_rims(source, extent):
    planes = source.shape[-2]
    lower_parts = []
    upper_parts = []
    for distance in range(1, -(-extent // planes) + 1):
        needed = min(planes, extent - (distance - 1) * planes)
        for heading in (1, -1):
            if heading == 1:
                outgoing = source[..., planes - needed :, :]
            else:
                outgoing = source[..., :needed, :]
            arrived = from_behind(outgoing, "space", heading * distance)
            if heading == 1:
                lower_parts.append(arrived)
            else:
                upper_parts.append(arrived)
    return jnp.concatenate(lower_parts[::-1] + [source] + upper_parts, axis=-2)


def dft_tables(length):
    indices = lax.iota(jnp.int32, length)
    product = indices[:, None] * indices[None, :] % length
    phases = 2.0 * math.pi / length * product.astype(jnp.float32)
    return (jnp.cos(phases), jnp.sin(phases))


def turn_axis(cosine, sines, values, pattern):
    direct = jnp.einsum(pattern, cosine, values, precision=lax.Precision.HIGHEST)
    crossed = jnp.einsum(pattern, sines, values, precision=lax.Precision.HIGHEST)
    real_part = direct[..., :NZ] - crossed[..., NZ:]
    imag_part = direct[..., NZ:] + crossed[..., :NZ]
    return jnp.concatenate([real_part, imag_part], axis=-1)


def squared_waves(length, anchor, extent):
    indices = anchor + lax.iota(jnp.int32, extent)
    signed = jnp.where(indices < (length + 1) // 2, indices, indices - length).astype(jnp.float32)
    return (2.0 * math.pi / length * signed) ** 2


def hartree_field(density):
    planes = density.shape[0]
    z_cosine, z_sine = dft_tables(NZ)
    y_cosine, y_sine = dft_tables(NY)
    x_cosine, x_sine = dft_tables(NX)
    forward_z = jnp.concatenate([z_cosine, -z_sine], axis=1)
    flattened = density.reshape(planes * NY, NZ)
    spectral = jnp.dot(
        flattened, forward_z, precision=lax.Precision.HIGHEST, preferred_element_type=jnp.float32
    )
    spectral = turn_axis(y_cosine, -y_sine, spectral.reshape(planes, NY, 2 * NZ), "ky,xyz->xkz")
    columns = lax.all_to_all(spectral, "space", split_axis=1, concat_axis=0, tiled=True)
    y_rows = columns.shape[1]
    spectral = turn_axis(x_cosine, -x_sine, columns, "kx,xyz->kyz")
    squares = (
        squared_waves(NX, 0, NX)[:, None, None]
        + squared_waves(NY, lax.axis_index("space") * y_rows, y_rows)[None, :, None]
        + squared_waves(NZ, 0, NZ)[None, None, :]
    )
    kernel = jnp.where(squares > 0, 4.0 * math.pi / jnp.where(squares > 0, squares, 1.0), 0.0)
    spectral = spectral * jnp.concatenate([kernel, kernel], axis=-1)
    spectral = turn_axis(x_cosine, x_sine, spectral, "kx,xyz->kyz")
    slabs = lax.all_to_all(spectral, "space", split_axis=0, concat_axis=1, tiled=True)
    spectral = turn_axis(y_cosine, y_sine, slabs, "ky,xyz->xkz")
    inverse_z = jnp.concatenate([z_cosine, -z_sine], axis=0)
    field_values = jnp.dot(
        spectral.reshape(planes * NY, 2 * NZ),
        inverse_z,
        precision=lax.Precision.HIGHEST,
        preferred_element_type=jnp.float32,
    )
    return (field_values / (NX * NY * NZ)).reshape(planes, NY * NZ)


def per_device_general(orbitals, potential, occupations):
    reach_cells = len(stencil_coeffs) - 1
    orbital_count = orbitals.shape[1]
    zero_copy = slab_rims(orbitals.astype(jnp.bfloat16), reach_cells)
    first_term = scaled_hamiltonian(orbitals, zero_copy, potential)
    first_copy = slab_rims(first_term.astype(jnp.bfloat16), reach_cells)
    second_term = 2.0 * scaled_hamiltonian(first_term, first_copy, potential) - orbitals
    prop_real = (
        bessel_terms[0] * orbitals[0]
        + 2.0 * bessel_terms[1] * first_term[1]
        - 2.0 * bessel_terms[2] * second_term[0]
    )
    prop_imag = (
        bessel_terms[0] * orbitals[1]
        - 2.0 * bessel_terms[1] * first_term[0]
        - 2.0 * bessel_terms[2] * second_term[1]
    )
    propagated = jnp.stack([prop_real, prop_imag])
    weights = occupations / (orbital_count * lax.axis_size("band"))
    partial_density = jnp.sum(
        weights[:, None, None] * (prop_real * prop_real + prop_imag * prop_imag), axis=0
    )
    density = lax.psum(partial_density, "band")
    hartree = hartree_field(density)
    return (propagated, density, hartree)


REACH = len(stencil_coeffs) - 1
TABLE_SCALE = 5040.0
CHUNK = 768
WINDOW = 1024
TILE = 256
MARGIN = 384


def plane_table():
    phases = CHUNK // TILE
    table = np.zeros((phases, WINDOW, TILE), np.float32)
    scaled = [round(coeff * TABLE_SCALE) for coeff in stencil_coeffs[1:]]
    for phase in range(phases):
        target = phase * TILE + np.arange(TILE)[None, :]
        origin = phase * TILE - MARGIN + np.arange(WINDOW)[:, None]
        y_step = origin // NZ - target // NZ
        z_step = origin % NZ - target % NZ
        for offset in range(1, REACH + 1):
            along_y = (np.abs(y_step) == offset) & (z_step == 0)
            along_z = (y_step == 0) & (np.abs(z_step) == offset)
            table[phase] += scaled[offset - 1] * (along_y | along_z)
    return jnp.asarray(table, jnp.bfloat16)


def joined(block, plane, lanes=slice(None)):
    return jnp.concatenate([block[0, plane, :, lanes], block[1, plane, :, lanes]], axis=0)


def rim_kernel(orbitals, lower, upper):
    step = pl.program_id(0)
    value = joined(orbitals, 0).astype(jnp.bfloat16)

    @pl.when(step < REACH)
    def _():
        lower[0] = value

    @pl.when(step >= REACH)
    def _():
        upper[0] = value


def rim_copies(moved):
    _, planes, count, cells = moved.shape
    rim = jax.ShapeDtypeStruct((REACH, 2 * count, cells), jnp.bfloat16)
    return pl.pallas_call(
        rim_kernel,
        grid=(2 * REACH,),
        in_specs=[
            pl.BlockSpec(
                (2, 1, count, cells),
                lambda i: (0, jnp.where(i < REACH, i, i + planes - 2 * REACH), 0, 0),
            )
        ],
        out_specs=[
            pl.BlockSpec((1, 2 * count, cells), lambda i: (jnp.minimum(i, REACH - 1), 0, 0)),
            pl.BlockSpec((1, 2 * count, cells), lambda i: (jnp.maximum(i - REACH, 0), 0, 0)),
        ],
        out_shape=[rim, rim],
        name="rim_copies",
    )(moved)


def center_factor(potential, plane, lanes):
    shift = energy_shift + 1.5 * stencil_coeffs[0]
    return (potential[plane : plane + 1, lanes] - shift) * (1.0 / energy_scale)


def across(values, plane, planes):
    total = None
    for offset in range(1, REACH + 1):
        pair = [values(at) for at in (plane - offset, plane + offset) if 0 <= at < planes]
        if pair:
            both = pair[0] + pair[1] if len(pair) == 2 else pair[0]
            term = (0.5 / energy_scale * stencil_coeffs[offset]) * both
            total = term if total is None else total + term
    return total


def first_kernel(current, left, right, potential, table, partial, to_lower, to_upper, copies, values):
    planes = current.shape[1]
    fields = 2 * current.shape[2]
    step = pl.program_id(0)
    last = pl.num_programs(0) - 1
    for plane in range(planes):
        rows = slice(fields * plane, fields * (plane + 1))
        own = joined(current, plane)
        values[rows, :] = own
        copies[rows, MARGIN : MARGIN + CHUNK] = own.astype(jnp.bfloat16)
        before = joined(left, plane)
        after = joined(right, plane)
        copies[rows, :MARGIN] = jnp.where(step == 0, 0.0, before).astype(jnp.bfloat16)
        copies[rows, MARGIN + CHUNK :] = jnp.where(step == last, 0.0, after).astype(jnp.bfloat16)
    for phase in range(CHUNK // TILE):
        lanes = slice(phase * TILE, (phase + 1) * TILE)
        in_plane = jnp.dot(
            copies[:, phase * TILE : phase * TILE + WINDOW], table[phase], preferred_element_type=jnp.float32
        )
        results = []
        for plane in range(planes):
            rows = slice(fields * plane, fields * (plane + 1))
            result = (
                center_factor(potential, plane, lanes) * values[rows, lanes]
                - (0.5 / energy_scale / TABLE_SCALE) * in_plane[rows]
                - across(lambda at: values[fields * at : fields * (at + 1), lanes], plane, planes)
            )
            partial[plane, :, lanes] = result
            results.append(result)
        for rim, into, order in ((to_upper, "up", results[::-1]), (to_lower, "down", results)):
            for plane in range(REACH):
                total = None
                for offset in range(plane + 1, REACH + 1):
                    term = stencil_coeffs[offset] * order[offset - plane - 1]
                    total = term if total is None else total + term
                rim[plane, :, lanes] = total.astype(jnp.bfloat16)


def first_partial(moved, potential, table):
    _, planes, count, cells = moved.shape
    chunks = cells // CHUNK
    margins = CHUNK // MARGIN
    fields = 2 * count
    rim = jax.ShapeDtypeStruct((REACH, fields, cells), jnp.bfloat16)
    rim_spec = pl.BlockSpec((REACH, fields, CHUNK), lambda i: (0, 0, i))
    return pl.pallas_call(
        first_kernel,
        grid=(chunks,),
        in_specs=[
            pl.BlockSpec((2, planes, count, CHUNK), lambda i: (0, 0, 0, i)),
            pl.BlockSpec((2, planes, count, MARGIN), lambda i: (0, 0, 0, jnp.maximum(margins * i - 1, 0))),
            pl.BlockSpec(
                (2, planes, count, MARGIN),
                lambda i: (0, 0, 0, jnp.minimum(margins * (i + 1), margins * chunks - 1)),
            ),
            pl.BlockSpec((planes, CHUNK), lambda i: (0, i)),
            pl.BlockSpec(table.shape, lambda i: (0, 0, 0)),
        ],
        out_specs=[pl.BlockSpec((planes, fields, CHUNK), lambda i: (0, 0, i)), rim_spec, rim_spec],
        out_shape=[jax.ShapeDtypeStruct((planes, fields, cells), jnp.float32), rim, rim],
        scratch_shapes=[
            pltpu.VMEM((planes * fields, CHUNK + 2 * MARGIN), jnp.bfloat16),
            pltpu.VMEM((planes * fields, CHUNK), jnp.float32),
        ],
        cost_estimate=pl.CostEstimate(flops=10**8, transcendentals=0, bytes_accessed=10**7),
        name="first_partial",
    )(moved, moved, moved, potential, table)


def rim_matrix():
    coeffs = stencil_coeffs
    matrix = np.zeros((REACH, REACH))
    for plane in range(REACH):
        for origin in range(REACH):
            for beyond in range(1, REACH + 1):
                if plane + beyond <= REACH and origin + beyond <= REACH:
                    matrix[plane, origin] -= 0.5 / energy_scale * coeffs[plane + beyond] * coeffs[origin + beyond]
    return matrix


def second_kernel(flags, partial, below, above, orbitals, potential, table, out, copies, firsts):
    planes = partial.shape[0]
    fields = partial.shape[1]
    cells = firsts.shape[1]
    step = pl.program_id(0)
    chunks = pl.num_programs(0) - 1
    half_scale = 0.5 / energy_scale

    @pl.when(step == 0)
    def _():
        copies[:, :MARGIN] = jnp.zeros((planes * fields, MARGIN), jnp.bfloat16)
        copies[:, MARGIN + cells :] = jnp.zeros((planes * fields, MARGIN), jnp.bfloat16)

    @pl.when(step < chunks)
    def _():
        base = pl.multiple_of(step * CHUNK, TILE)
        for plane in range(planes):
            rows = slice(fields * plane, fields * (plane + 1))
            first = partial[plane]
            for offset in range(1, REACH + 1):
                if plane - offset < 0:
                    first = first - half_scale * stencil_coeffs[offset] * below[REACH + plane - offset].astype(jnp.float32)
                if plane + offset >= planes:
                    first = first - half_scale * stencil_coeffs[offset] * above[plane + offset - planes].astype(jnp.float32)
            firsts[rows, pl.ds(base, CHUNK)] = first
            copies[rows, pl.ds(pl.multiple_of(base + MARGIN, 128), CHUNK)] = first.astype(jnp.bfloat16)

    @pl.when(step > 0)
    def _():
        base = pl.multiple_of((step - 1) * CHUNK, TILE)
        rim = rim_matrix()
        row = lax.broadcasted_iota(jnp.int32, (fields, TILE), 0)
        turn = jnp.where(row < fields // 2, 2.0 * bessel_terms[1], -2.0 * bessel_terms[1])
        for phase in range(CHUNK // TILE):
            start = pl.multiple_of(base + phase * TILE, TILE)
            lanes = slice(phase * TILE, (phase + 1) * TILE)
            in_plane = jnp.dot(copies[:, pl.ds(start, WINDOW)], table[phase], preferred_element_type=jnp.float32)
            origin = [joined(orbitals, plane, lanes) for plane in range(planes)]
            first = [firsts[fields * plane : fields * (plane + 1), pl.ds(start, TILE)] for plane in range(planes)]
            for plane in range(planes):
                rows = slice(fields * plane, fields * (plane + 1))
                energy = (
                    center_factor(potential, plane, lanes) * first[plane]
                    - (half_scale / TABLE_SCALE) * in_plane[rows]
                    - across(lambda at: first[at], plane, planes)
                )
                result = (
                    (bessel_terms[0] + 2.0 * bessel_terms[2]) * origin[plane]
                    + turn * pltpu.roll(first[plane], fields // 2, 0)
                    - (4.0 * bessel_terms[2]) * energy
                )
                gain = 4.0 * bessel_terms[2] * half_scale
                if plane < REACH:
                    total = sum(float(gain * rim[plane, at]) * origin[at] for at in range(REACH))
                    result = result + flags[0] * total
                mirrored = planes - 1 - plane
                if mirrored < REACH:
                    total = sum(float(gain * rim[mirrored, at]) * origin[planes - 1 - at] for at in range(REACH))
                    result = result + flags[1] * total
                out[plane, :, lanes] = result


def second_partial(flags, partial, below, above, moved, potential, table):
    _, planes, count, cells = moved.shape
    chunks = cells // CHUNK
    fields = 2 * count
    ahead = lambda i: jnp.minimum(i, chunks - 1)
    behind = lambda i: jnp.maximum(i - 1, 0)
    rim_spec = pl.BlockSpec((REACH, fields, CHUNK), lambda i: (0, 0, ahead(i)))
    return pl.pallas_call(
        second_kernel,
        grid=(chunks + 1,),
        in_specs=[
            pl.BlockSpec(memory_space=pltpu.SMEM),
            pl.BlockSpec((planes, fields, CHUNK), lambda i: (0, 0, ahead(i))),
            rim_spec,
            rim_spec,
            pl.BlockSpec((2, planes, count, CHUNK), lambda i: (0, 0, 0, behind(i))),
            pl.BlockSpec((planes, CHUNK), lambda i: (0, behind(i))),
            pl.BlockSpec(table.shape, lambda i: (0, 0, 0)),
        ],
        out_specs=pl.BlockSpec((planes, fields, CHUNK), lambda i: (0, 0, behind(i))),
        out_shape=jax.ShapeDtypeStruct((planes, fields, cells), jnp.float32),
        scratch_shapes=[
            pltpu.VMEM((planes * fields, cells + 2 * MARGIN), jnp.bfloat16),
            pltpu.VMEM((planes * fields, cells), jnp.float32),
        ],
        cost_estimate=pl.CostEstimate(flops=10**8, transcendentals=0, bytes_accessed=10**7),
        name="second_partial",
    )(flags, partial, below, above, moved, potential, table)


def finish_kernel(partial, below, above, weights, out, density):
    planes = partial.shape[0]
    count = out.shape[2]
    gain = 4.0 * bessel_terms[2] * 0.5 / energy_scale
    weight = weights[:, :1]
    for plane in range(planes):
        value = partial[plane]
        if plane < REACH:
            value = value + gain * below[plane].astype(jnp.float32)
        if planes - 1 - plane < REACH:
            value = value + gain * above[planes - 1 - plane].astype(jnp.float32)
        out[0, plane] = value[:count]
        out[1, plane] = value[count:]
        density[plane : plane + 1, :] = jnp.sum(weight * (value * value), axis=0, keepdims=True)


def finish(partial, below, above, weights):
    planes, fields, cells = partial.shape
    chunks = cells // CHUNK
    rim_spec = pl.BlockSpec((REACH, fields, CHUNK), lambda i: (0, 0, i))
    return pl.pallas_call(
        finish_kernel,
        grid=(chunks,),
        in_specs=[
            pl.BlockSpec((planes, fields, CHUNK), lambda i: (0, 0, i)),
            rim_spec,
            rim_spec,
            pl.BlockSpec((fields, 128), lambda i: (0, 0)),
        ],
        out_specs=[
            pl.BlockSpec((2, planes, fields // 2, CHUNK), lambda i: (0, 0, 0, i)),
            pl.BlockSpec((planes, CHUNK), lambda i: (0, i)),
        ],
        out_shape=[
            jax.ShapeDtypeStruct((2, planes, fields // 2, cells), jnp.float32),
            jax.ShapeDtypeStruct((planes, cells), jnp.float32),
        ],
        name="finish",
    )(partial, below, above, weights)


def wave_basis(length):
    cells = np.arange(length)
    rows = []
    waves = []
    for wave in range(length // 2 + 1):
        norm = math.sqrt((1.0 if wave in (0, length / 2) else 2.0) / length)
        rows.append(norm * np.cos(2.0 * math.pi / length * (wave * cells % length)))
        waves.append(wave)
    for wave in range(1, (length + 1) // 2):
        rows.append(math.sqrt(2.0 / length) * np.sin(2.0 * math.pi / length * (wave * cells % length)))
        waves.append(wave)
    return np.asarray(rows, np.float32), (2.0 * math.pi / length * np.asarray(waves, np.float64)) ** 2


def hartree_waves(partial_density):
    planes = partial_density.shape[0]
    bands = lax.axis_size("band")
    blocks = lax.axis_size("space")
    whole = ("band", "space")
    exact = dict(precision=lax.Precision.HIGHEST, preferred_element_type=jnp.float32)
    z_basis, z_squares = wave_basis(NZ)
    y_basis, y_squares = wave_basis(NY)
    x_basis, x_squares = wave_basis(planes * blocks)
    grid = partial_density.reshape(planes, NY, NZ)
    spectral = jnp.einsum("xyz,cz->xyc", grid, z_basis, **exact)
    spectral = jnp.einsum("by,xyc->xbc", y_basis, spectral, **exact)
    columns = lax.all_to_all(spectral, whole, split_axis=1, concat_axis=0, tiled=True)
    rows = columns.shape[1]
    columns = jnp.sum(columns.reshape(bands, planes * blocks, rows, NZ), axis=0)
    place = (lax.axis_index("band") * blocks + lax.axis_index("space")) * rows
    squares = (
        jnp.asarray(x_squares, jnp.float32)[:, None, None]
        + lax.dynamic_slice_in_dim(jnp.asarray(y_squares, jnp.float32), place, rows)[None, :, None]
        + jnp.asarray(z_squares, jnp.float32)[None, None, :]
    )
    kernel = jnp.where(squares > 0, 4.0 * math.pi / jnp.where(squares > 0, squares, 1.0), 0.0)
    columns = jnp.einsum("ax,xbc->abc", x_basis, columns, **exact) * kernel
    columns = jnp.einsum("ax,abc->xbc", x_basis, columns, **exact)
    spread = jnp.broadcast_to(columns[None], (bands, *columns.shape)).reshape(-1, rows, NZ)
    spectral = lax.all_to_all(spread, whole, split_axis=0, concat_axis=1, tiled=True)
    spectral = jnp.einsum("by,xbc->xyc", y_basis, spectral, **exact)
    field = jnp.einsum("cz,xyc->xyz", z_basis, spectral, **exact)
    return field.reshape(planes, NY * NZ)


def ring_shift(x, axis, by):
    count = lax.axis_size(axis)
    return lax.ppermute(x, axis, [(i, (i + by) % count) for i in range(count)])


def band_sum(partial):
    bands = lax.axis_size("band")
    mine = lax.axis_index("band")
    width = partial.shape[1] // bands
    piece = lambda shift: lax.dynamic_slice_in_dim(partial, (mine + shift) % bands * width, width, 1)
    own = piece(0)
    for shift in range(1, bands):
        own = own + ring_shift(piece(shift), "band", shift)
    total = jnp.zeros_like(partial)
    total = lax.dynamic_update_slice_in_dim(total, own, mine * width, 1)
    for shift in range(1, bands):
        arrived = ring_shift(own, "band", shift)
        total = lax.dynamic_update_slice_in_dim(total, arrived, (mine - shift) % bands * width, 1)
    return total


def per_device_blocks(orbitals, potential, occupations):
    count = orbitals.shape[1]
    moved = orbitals.transpose(0, 2, 1, 3)
    table = plane_table()
    place = lax.axis_index("space")
    flags = jnp.stack([place > 0, place < lax.axis_size("space") - 1]).astype(jnp.float32)
    lower, upper = rim_copies(moved)
    below = from_behind(upper, "space", 1)
    above = from_behind(lower, "space", -1)
    partial, to_lower, to_upper = first_partial(moved, potential, table)
    terms_below = from_behind(to_upper, "space", 1)
    terms_above = from_behind(to_lower, "space", -1)
    partial = second_partial(flags, partial, below, above, moved, potential, table)
    weights = occupations / (count * lax.axis_size("band"))
    weights = jnp.broadcast_to(jnp.concatenate([weights, weights])[:, None], (2 * count, 128))
    propagated, partial_density = finish(partial, terms_below, terms_above, weights)
    hartree = hartree_waves(partial_density)
    density = band_sum(partial_density)
    return (propagated.transpose(0, 2, 1, 3), density, hartree)


def per_device(orbitals, potential, occupations):
    _, count, planes, cells = orbitals.shape
    columns = NY % (lax.axis_size("space") * lax.axis_size("band"))
    if planes < 2 * REACH or count != 4 or cells % CHUNK or CHUNK % NZ or MARGIN != REACH * NZ or columns:
        return per_device_general(orbitals, potential, occupations)
    return per_device_blocks(orbitals, potential, occupations)


def solution(mesh):
    in_specs = (P(None, "band", "space", None), P("space", None), P("band"))
    out_specs = (P(None, "band", "space", None), P("space", None), P("space", None))
    return jax.shard_map(
        per_device, mesh=mesh, in_specs=in_specs, out_specs=out_specs, check_vma=False
    )
```

profile of v0, /device:TPU:0, one launch (start us, length us, event | category | flops | bytes accessed | tf_op | source)
XLA Modules:
  0.0 131.4 jit_solution(10945944281442358626)
XLA Ops:
  0.6 5.7 %rim_copies.1 = (bf16[4,8,9216]{2,1,0:T(8,128)(2,1)}, bf16[4,8,9216]{2,1,0:T(8,128)(2,1)}) custom-call(f32[2,12,4,9216]{3,2,1,0:T(4,128)} %bitcast.33), custom_call_target="tpu_custom_call" | custom-call | tf_op jit(solution)/shard_map/rim_copies/pallas_call | solution.py:207
  6.3 2.4 %collective-permute-start = (bf16[4,8,9216]{2,1,0:T(8,128)(2,1)}, bf16[4,8,9216]{2,1,0:T(8,128)(2,1)S(1)}, u32[]{:S(2)}, u32[]{:S(2)}) collective-permute-start(bf16[4,8,9216]{2,1,0:T(8,128)(2,1)} %get-tuple-element.11), channel_id=1, source_target_pairs={{0,1},{1,2},{2,3},{3,4},{4,5},{5,6},{6,7},{8,9},{9,10},{10,11},{11... | collective-permute-start | bytes 1769480 | tf_op jit(solution)/shard_map/ppermute | solution.py:25
  8.7 0.0 copy-start.6
  8.8 1.3 collective-permute-start.1
  10.1 11.9 %first_partial.1 = (f32[12,8,9216]{2,1,0:T(8,128)}, bf16[4,8,9216]{2,1,0:T(8,128)(2,1)}, bf16[4,8,9216]{2,1,0:T(8,128)(2,1)}) custom-call(f32[2,12,4,9216]{3,2,1,0:T(4,128)} %bitcast.34, f32[2,12,4,9216]{3,2,1,0:T(4,128)} %bitcast.35, f32[2,12,4,9216]{3,2,1,0:T(4,128)} %bitcast.36, f32[12,9216]{1,0:T(8,128)} %potential.3, ...), custom_call_target="tpu_custom_call" | custom-call | flops 100000000 | bytes 10000000 | tf_op jit(solution)/shard_map/first_partial/pallas_call | solution.py:286
  22.0 5.1 %collective-permute-start.2 = (bf16[4,8,9216]{2,1,0:T(8,128)(2,1)}, bf16[4,8,9216]{2,1,0:T(8,128)(2,1)S(1)}, u32[]{:S(2)}, u32[]{:S(2)}) collective-permute-start(bf16[4,8,9216]{2,1,0:T(8,128)(2,1)} %get-tuple-element.13), channel_id=1, source_target_pairs={{0,1},{1,2},{2,3},{3,4},{4,5},{5,6},{6,7},{8,9},{9,10},{10,11},{11... | collective-permute-start | bytes 1769480 | tf_op jit(solution)/shard_map/ppermute | solution.py:25
  27.1 1.3 collective-permute-start.3
  28.4 0.1 dynamic_slice.19
  28.5 0.1 pad_maximum_fusion
  28.6 0.7 add_convert_fusion.flags
  29.3 0.8 copy-done.1
  30.1 0.2 copy-done.2
  30.3 13.2 %second_partial.1.partial = f32[12,8,9216]{2,1,0:T(8,128)} custom-call(f32[2]{0:T(128)} %add_convert_fusion.flags, f32[12,8,9216]{2,1,0:T(8,128)} %get-tuple-element.10.partial, bf16[4,8,9216]{2,1,0:T(8,128)(2,1)} %copy-done.1, bf16[4,8,9216]{2,1,0:T(8,128)(2,1)} %copy-done.2, f32[2,12,4,9216]{3,2,1,0:T(4,128)} %bitcast.37, f32[12,9216]{1,0:T(8,128)} %potential.3, ...), custom_call_target="tpu_custom_call" | custom-call | flops 100000000 | bytes 10000000 | tf_op jit(solution)/shard_map/second_partial/pallas_call | solution.py:390
  43.5 0.0 copy-start.4
  43.5 0.8 broadcast_in_dim.11.weights
  44.3 0.0 copy-done.4
  44.3 0.2 copy-done.5
  44.5 9.1 %finish.1 = (f32[2,12,4,9216]{3,2,1,0:T(4,128)}, f32[12,9216]{1,0:T(8,128)}) custom-call(f32[12,8,9216]{2,1,0:T(8,128)} %second_partial.1.partial, bf16[4,8,9216]{2,1,0:T(8,128)(2,1)} %copy-done.4, bf16[4,8,9216]{2,1,0:T(8,128)(2,1)} %copy-done.5, f32[8,128]{1,0:T(8,128)} %broadcast_in_dim.11.weights), custom_call_target="tpu_custom_call" | custom-call | tf_op jit(solution)/shard_map/finish/pallas_call | solution.py:433
  53.6 1.3 reshape.54
  54.9 1.1 constant_dynamic-slice_fusion.2
  56.0 3.7 %collective-permute-start.6 = (f32[12,2304]{1,0:T(8,128)S(1)}, f32[12,2304]{1,0:T(8,128)S(1)}, u32[]{:S(2)}, u32[]{:S(2)}) collective-permute-start(f32[12,2304]{1,0:T(8,128)S(1)} %get-tuple-element.20), channel_id=1, source_target_pairs={{0,24},{8,0},{16,8},{24,16},{1,25},{9,1},{17,9},{25,17},{2,26},{10... | collective-permute-start | bytes 331784 | tf_op jit(solution)/shard_map/ppermute | solution.py:501
  59.6 1.0 collective-permute-start.4
  60.7 1.4 %fusion.2 = f32[12,96,96]{1,2,0:T(8,128)S(1)} fusion(f32[12,96,96]{2,1,0:T(8,128)S(1)} %reshape.54, f32[96,96,1]{1,0,2:T(8,128)S(1)} %copy-done), kind=kOutput, calls=%fused_computation.21 | convolution fusion | flops 127401984 | bytes 921600 | tf_op jit(solution)/shard_map/xyz,cz->xyc/dot_general | solution.py:478
  62.1 0.6 convolution_bitcast_fusion.1
  62.7 1.2 copy.30
  63.9 8.4 %all-to-all-start = ((f32[12,96,96]{2,0,1:T(8,128)}), f32[12,96,96]{2,0,1:T(8,128)S(1)}, u32[]{:S(2)}, u32[]{:S(2)}) async-start(f32[12,96,96]{2,0,1:T(8,128)} %copy.30), calls=%async_computation | async-start | bytes 1572864 | tf_op jit(solution)/shard_map/all_to_all | solution.py:480
  72.3 0.1 broadcast_add_fusion
  72.4 0.3 collective-permute-done.5
  72.8 1.0 constant_dynamic-update-slice_fusion.3
  73.7 1.6 %collective-permute-start.7 = (f32[12,2304]{1,0:T(8,128)S(1)}, f32[12,2304]{1,0:T(8,128)S(1)}, u32[]{:S(2)}, u32[]{:S(2)}) collective-permute-start(f32[12,2304]{1,0:T(8,128)S(1)} %get-tuple-element.18), channel_id=1, source_target_pairs={{0,8},{8,16},{16,24},{24,0},{1,9},{9,17},{17,25},{25,1},{2,10},{10... | collective-permute-start | bytes 331784 | tf_op jit(solution)/shard_map/ppermute | solution.py:501
  75.3 2.4 %collective-permute-start.8 = (f32[12,2304]{1,0:T(8,128)S(1)}, f32[12,2304]{1,0:T(8,128)S(1)}, u32[]{:S(2)}, u32[]{:S(2)}) collective-permute-start(f32[12,2304]{1,0:T(8,128)S(1)} %get-tuple-element.18), channel_id=1, source_target_pairs={{0,16},{8,24},{16,0},{24,8},{1,17},{9,25},{17,1},{25,9},{2,18},{10... | collective-permute-start | bytes 331784 | tf_op jit(solution)/shard_map/ppermute | solution.py:501
  77.7 2.0 %collective-permute-start.9 = (f32[12,2304]{1,0:T(8,128)S(1)}, f32[12,2304]{1,0:T(8,128)S(1)}, u32[]{:S(2)}, u32[]{:S(2)}) collective-permute-start(f32[12,2304]{1,0:T(8,128)S(1)} %get-tuple-element.18), channel_id=1, source_target_pairs={{0,24},{8,0},{16,8},{24,16},{1,25},{9,1},{17,9},{25,17},{2,26},{10... | collective-permute-start | bytes 331784 | tf_op jit(solution)/shard_map/ppermute | solution.py:501
  79.7 20.1 %all-to-all-done = f32[12,96,96]{2,0,1:T(8,128)S(1)} async-done(((f32[12,96,96]{2,0,1:T(8,128)}), f32[12,96,96]{2,0,1:T(8,128)S(1)}, u32[]{:S(2)}, u32[]{:S(2)}) %all-to-all-start) | async-done | bytes 442400 | tf_op jit(solution)/shard_map/all_to_all | solution.py:480
  99.8 0.3 copy.49
  100.1 0.4 copy.32
  100.5 0.1 reshape.55
  100.6 0.3 convolution_multiply_fusion
  100.9 0.3 fusion.3
  101.2 0.1 copy.34
  101.3 1.0 broadcast_in_dim.26
  102.3 4.3 %all-to-all-start.1 = ((f32[384,3,96]{2,1,0:T(4,128)}), f32[384,3,96]{2,1,0:T(4,128)S(1)}, u32[]{:S(2)}, u32[]{:S(2)}) async-start(f32[384,3,96]{2,1,0:T(4,128)} %bitcast.9), calls=%async_computation.1 | async-start | bytes 1572864 | tf_op jit(solution)/shard_map/all_to_all | solution.py:493
  106.8 20.5 %all-to-all-done.1 = f32[384,3,96]{2,1,0:T(4,128)S(1)} async-done(((f32[384,3,96]{2,1,0:T(4,128)}), f32[384,3,96]{2,1,0:T(4,128)S(1)}, u32[]{:S(2)}, u32[]{:S(2)}) %all-to-all-start.1) | async-done | bytes 442400 | tf_op jit(solution)/shard_map/all_to_all | solution.py:493
  127.2 0.1 copy.48
  127.3 0.4 copy.36
  127.7 0.3 all_to_all.30
  128.0 1.1 convolution_bitcast_fusion
  129.1 1.1 fusion.4
  130.2 1.2 reshape.57
  (26 shorter events, 0.2 us)
Async XLA Ops:
  6.3 23.0 %collective-permute-start = (bf16[4,8,9216]{2,1,0:T(8,128)(2,1)}, bf16[4,8,9216]{2,1,0:T(8,128)(2,1)S(1)}, u32[]{:S(2)}, u32[]{:S(2)}) collective-permute-start(bf16[4,8,9216]{2,1,0:T(8,128)(2,1)} %get-tuple-element.11), channel_id=1, source_target_pairs={{0,1},{1,2},{2,3},{3,4},{4,5},{5,6},{6,7},{8,9},{9,10},{10,11},{11... | collective-permute-start | bytes 1769480 | tf_op jit(solution)/shard_map/ppermute | solution.py:25
  8.7 19.7 %copy-start.6 = (f32[96]{0:T(128)S(1)}, f32[96]{0:T(128)}, u32[]{:S(2)}) copy-start(f32[96]{0:T(128)} %constant.86.clone) | copy-start | bytes 1156
  8.7 19.8 %copy-start.7 = (f32[4]{0:T(128)S(1)}, f32[4]{0:T(128)}, u32[]{:S(2)}) copy-start(f32[4]{0:T(128)} %param.15) | copy-start | bytes 52
  8.8 20.5 %collective-permute-start.1 = (bf16[4,8,9216]{2,1,0:T(8,128)(2,1)}, bf16[4,8,9216]{2,1,0:T(8,128)(2,1)S(1)}, u32[]{:S(2)}, u32[]{:S(2)}) collective-permute-start(bf16[4,8,9216]{2,1,0:T(8,128)(2,1)} %get-tuple-element.12), channel_id=1, source_target_pairs={{1,0},{2,1},{3,2},{4,3},{5,4},{6,5},{7,6},{9,8},{10,9},{11,10},{12... | collective-permute-start | bytes 1769480 | tf_op jit(solution)/shard_map/ppermute | solution.py:25
  22.0 21.5 %collective-permute-start.2 = (bf16[4,8,9216]{2,1,0:T(8,128)(2,1)}, bf16[4,8,9216]{2,1,0:T(8,128)(2,1)S(1)}, u32[]{:S(2)}, u32[]{:S(2)}) collective-permute-start(bf16[4,8,9216]{2,1,0:T(8,128)(2,1)} %get-tuple-element.13), channel_id=1, source_target_pairs={{0,1},{1,2},{2,3},{3,4},{4,5},{5,6},{6,7},{8,9},{9,10},{10,11},{11... | collective-permute-start | bytes 1769480 | tf_op jit(solution)/shard_map/ppermute | solution.py:25
  27.1 16.4 %collective-permute-start.3 = (bf16[4,8,9216]{2,1,0:T(8,128)(2,1)}, bf16[4,8,9216]{2,1,0:T(8,128)(2,1)S(1)}, u32[]{:S(2)}, u32[]{:S(2)}) collective-permute-start(bf16[4,8,9216]{2,1,0:T(8,128)(2,1)} %get-tuple-element.14), channel_id=1, source_target_pairs={{1,0},{2,1},{3,2},{4,3},{5,4},{6,5},{7,6},{9,8},{10,9},{11,10},{12... | collective-permute-start | bytes 1769480 | tf_op jit(solution)/shard_map/ppermute | solution.py:25
  29.3 0.8 copy-start.1
  29.3 1.0 copy-start.2
  43.5 17.2 %copy-start = (f32[96,96,1]{1,0,2:T(8,128)S(1)}, f32[96,96,1]{1,0,2:T(8,128)}, u32[]{:S(2)}) copy-start(f32[96,96,1]{1,0,2:T(8,128)} %constant.89) | copy-start | bytes 110596
  43.5 0.8 copy-start.4
  43.5 1.0 copy-start.5
  56.0 16.4 %collective-permute-start.6 = (f32[12,2304]{1,0:T(8,128)S(1)}, f32[12,2304]{1,0:T(8,128)S(1)}, u32[]{:S(2)}, u32[]{:S(2)}) collective-permute-start(f32[12,2304]{1,0:T(8,128)S(1)} %get-tuple-element.20), channel_id=1, source_target_pairs={{0,24},{8,0},{16,8},{24,16},{1,25},{9,1},{17,9},{25,17},{2,26},{10... | collective-permute-start | bytes 331784 | tf_op jit(solution)/shard_map/ppermute | solution.py:501
  59.6 13.1 %collective-permute-start.5 = (f32[12,2304]{1,0:T(8,128)S(1)}, f32[12,2304]{1,0:T(8,128)S(1)}, u32[]{:S(2)}, u32[]{:S(2)}) collective-permute-start(f32[12,2304]{1,0:T(8,128)S(1)} %get-tuple-element.21), channel_id=1, source_target_pairs={{0,16},{8,24},{16,0},{24,8},{1,17},{9,25},{17,1},{25,9},{2,18},{10... | collective-permute-start | bytes 331784 | tf_op jit(solution)/shard_map/ppermute | solution.py:501
  59.6 13.1 %collective-permute-start.4 = (f32[12,2304]{1,0:T(8,128)S(1)}, f32[12,2304]{1,0:T(8,128)S(1)}, u32[]{:S(2)}, u32[]{:S(2)}) collective-permute-start(f32[12,2304]{1,0:T(8,128)S(1)} %get-tuple-element.19), channel_id=1, source_target_pairs={{0,8},{8,16},{16,24},{24,0},{1,9},{9,17},{17,25},{25,1},{2,10},{10... | collective-permute-start | bytes 331784 | tf_op jit(solution)/shard_map/ppermute | solution.py:501
  63.9 35.9 %all-to-all-start = ((f32[12,96,96]{2,0,1:T(8,128)}), f32[12,96,96]{2,0,1:T(8,128)S(1)}, u32[]{:S(2)}, u32[]{:S(2)}) async-start(f32[12,96,96]{2,0,1:T(8,128)} %copy.30), calls=%async_computation | async-start | bytes 1572864 | tf_op jit(solution)/shard_map/all_to_all | solution.py:480
  73.7 32.9 %collective-permute-start.7 = (f32[12,2304]{1,0:T(8,128)S(1)}, f32[12,2304]{1,0:T(8,128)S(1)}, u32[]{:S(2)}, u32[]{:S(2)}) collective-permute-start(f32[12,2304]{1,0:T(8,128)S(1)} %get-tuple-element.18), channel_id=1, source_target_pairs={{0,8},{8,16},{16,24},{24,0},{1,9},{9,17},{17,25},{25,1},{2,10},{10... | collective-permute-start | bytes 331784 | tf_op jit(solution)/shard_map/ppermute | solution.py:501
  75.3 31.4 %collective-permute-start.8 = (f32[12,2304]{1,0:T(8,128)S(1)}, f32[12,2304]{1,0:T(8,128)S(1)}, u32[]{:S(2)}, u32[]{:S(2)}) collective-permute-start(f32[12,2304]{1,0:T(8,128)S(1)} %get-tuple-element.18), channel_id=1, source_target_pairs={{0,16},{8,24},{16,0},{24,8},{1,17},{9,25},{17,1},{25,9},{2,18},{10... | collective-permute-start | bytes 331784 | tf_op jit(solution)/shard_map/ppermute | solution.py:501
  77.7 29.0 %collective-permute-start.9 = (f32[12,2304]{1,0:T(8,128)S(1)}, f32[12,2304]{1,0:T(8,128)S(1)}, u32[]{:S(2)}, u32[]{:S(2)}) collective-permute-start(f32[12,2304]{1,0:T(8,128)S(1)} %get-tuple-element.18), channel_id=1, source_target_pairs={{0,24},{8,0},{16,8},{24,16},{1,25},{9,1},{17,9},{25,17},{2,26},{10... | collective-permute-start | bytes 331784 | tf_op jit(solution)/shard_map/ppermute | solution.py:501
  102.3 24.9 %all-to-all-start.1 = ((f32[384,3,96]{2,1,0:T(4,128)}), f32[384,3,96]{2,1,0:T(4,128)S(1)}, u32[]{:S(2)}, u32[]{:S(2)}) async-start(f32[384,3,96]{2,1,0:T(4,128)} %bitcast.9), calls=%async_computation.1 | async-start | bytes 1572864 | tf_op jit(solution)/shard_map/all_to_all | solution.py:493
  106.8 24.6 %copy-start.3 = (f32[12,9216]{1,0:T(8,128)}, f32[12,9216]{1,0:T(8,128)S(1)}, u32[]{:S(2)}) copy-start(f32[12,9216]{1,0:T(8,128)S(1)} %constant_dynamic-update-slice_fusion) | copy-start | bytes 1327108
where the time goes:
time: 133 us; the launch traced here: 131 us
  waiting for transfers between devices  40.9 us (31%)
  Pallas kernels  39.8 us (30%)
  starting transfers between devices  33.5 us (25%)
  local copies, waits for them, and re-layouts  9.51 us (7%)
  matrix products  4.83 us (4%)
  other arithmetic  1.8 us (1%)
    all_to_all x1, waiting for transfers between devices, hartree_waves(): lax.all_to_all(spread, whole, split_axis=0, concat_axis=1, tiled=True)  20.5 us
    all_to_all x1, waiting for transfers between devices, hartree_waves(): lax.all_to_all(spectral, whole, split_axis=1, concat_axis=0, tiled=True)  20.1 us
    pallas_call x1, Pallas kernels, second_partial(): pl.pallas_call(second_kernel, grid=(chunks + 1,), in_specs=[pl.BlockSpec(...  13.2 us
    pallas_call x1, Pallas kernels, first_partial(): pl.pallas_call(first_kernel, grid=(chunks,), in_specs=[pl.BlockSpec((2, p...  11.9 us
    ppermute x6, starting transfers between devices, ring_shift(): return lax.ppermute(x, axis, [(i, (i + by) % count) for i in range(count)])  10.7 us
    ppermute x4, starting transfers between devices, from_behind(): return lax.ppermute(x, axis, pairs)  10.1 us
    pallas_call x1, Pallas kernels, finish(): pl.pallas_call(finish_kernel, grid=(chunks,), in_specs=[pl.BlockSpec((pla...  9.11 us
    all_to_all x1, starting transfers between devices, hartree_waves(): lax.all_to_all(spectral, whole, split_axis=1, concat_axis=0, tiled=True)  8.39 us
  transfers between devices with their start and end apart: 12, of which 3 were waited for; matrix products, arithmetic and copies ran while one was open for 6% of the time, Pallas kernels for 19%

commit v1 on v0

--- a/solution.py
+++ b/solution.py
@@ -162,14 +162,15 @@
 
 REACH = len(stencil_coeffs) - 1
 TABLE_SCALE = 5040.0
-CHUNK = 768
+PERIOD = 768
+CHUNK = 2304
 WINDOW = 1024
 TILE = 256
 MARGIN = 384
 
 
 def plane_table():
-    phases = CHUNK // TILE
+    phases = PERIOD // TILE
     table = np.zeros((phases, WINDOW, TILE), np.float32)
     scaled = [round(coeff * TABLE_SCALE) for coeff in stencil_coeffs[1:]]
     for phase in range(phases):
@@ -188,17 +189,19 @@
     return jnp.concatenate([block[0, plane, :, lanes], block[1, plane, :, lanes]], axis=0)
 
 
-def rim_kernel(orbitals, lower, upper):
-    step = pl.program_id(0)
-    value = joined(orbitals, 0).astype(jnp.bfloat16)
-
-    @pl.when(step < REACH)
-    def _():
-        lower[0] = value
-
-    @pl.when(step >= REACH)
-    def _():
-        upper[0] = value
+def rim_kernel(orbitals, lower, upper, staged, arrivals):
+    planes = orbitals.shape[1]
+    starts = (0, planes - REACH)
+    copies = [
+        pltpu.make_async_copy(orbitals.at[:, pl.ds(start, REACH)], staged.at[side], arrivals.at[side])
+        for side, start in enumerate(starts)
+    ]
+    for copy in copies:
+        copy.start()
+    for side, rim in enumerate((lower, upper)):
+        copies[side].wait()
+        for plane in range(REACH):
+            rim[plane] = jnp.concatenate([staged[side, 0, plane], staged[side, 1, plane]], axis=0).astype(jnp.bfloat16)
 
 
 def rim_copies(moved):
@@ -206,18 +209,13 @@
     rim = jax.ShapeDtypeStruct((REACH, 2 * count, cells), jnp.bfloat16)
     return pl.pallas_call(
         rim_kernel,
-        grid=(2 * REACH,),
-        in_specs=[
-            pl.BlockSpec(
-                (2, 1, count, cells),
-                lambda i: (0, jnp.where(i < REACH, i, i + planes - 2 * REACH), 0, 0),
-            )
-        ],
-        out_specs=[
-            pl.BlockSpec((1, 2 * count, cells), lambda i: (jnp.minimum(i, REACH - 1), 0, 0)),
-            pl.BlockSpec((1, 2 * count, cells), lambda i: (jnp.maximum(i - REACH, 0), 0, 0)),
-        ],
+        in_specs=[pl.BlockSpec(memory_space=pl.ANY)],
+        out_specs=[pl.BlockSpec(memory_space=pltpu.VMEM)] * 2,
         out_shape=[rim, rim],
+        scratch_shapes=[
+            pltpu.VMEM((2, 2, REACH, count, cells), jnp.float32),
+            pltpu.SemaphoreType.DMA((2,)),
+        ],
         name="rim_copies",
     )(moved)
 
@@ -255,7 +253,7 @@
     for phase in range(CHUNK // TILE):
         lanes = slice(phase * TILE, (phase + 1) * TILE)
         in_plane = jnp.dot(
-            copies[:, phase * TILE : phase * TILE + WINDOW], table[phase], preferred_element_type=jnp.float32
+            copies[:, phase * TILE : phase * TILE + WINDOW], table[phase % (PERIOD // TILE)], preferred_element_type=jnp.float32
         )
         results = []
         for plane in range(planes):
@@ -318,13 +316,15 @@
     return matrix
 
 
-def second_kernel(flags, partial, below, above, orbitals, potential, table, out, copies, firsts):
+def second_kernel(partial, below, above, orbitals, potential, table, out, copies, firsts):
     planes = partial.shape[0]
     fields = partial.shape[1]
     cells = firsts.shape[1]
     step = pl.program_id(0)
     chunks = pl.num_programs(0) - 1
     half_scale = 0.5 / energy_scale
+    place = lax.axis_index("space")
+    flags = [(place > 0).astype(jnp.float32), (place < lax.axis_size("space") - 1).astype(jnp.float32)]
 
     @pl.when(step == 0)
     def _():
@@ -354,7 +354,7 @@
         for phase in range(CHUNK // TILE):
             start = pl.multiple_of(base + phase * TILE, TILE)
             lanes = slice(phase * TILE, (phase + 1) * TILE)
-            in_plane = jnp.dot(copies[:, pl.ds(start, WINDOW)], table[phase], preferred_element_type=jnp.float32)
+            in_plane = jnp.dot(copies[:, pl.ds(start, WINDOW)], table[phase % (PERIOD // TILE)], preferred_element_type=jnp.float32)
             origin = [joined(orbitals, plane, lanes) for plane in range(planes)]
             first = [firsts[fields * plane : fields * (plane + 1), pl.ds(start, TILE)] for plane in range(planes)]
             for plane in range(planes):
@@ -380,7 +380,7 @@
                 out[plane, :, lanes] = result
 
 
-def second_partial(flags, partial, below, above, moved, potential, table):
+def second_partial(partial, below, above, moved, potential, table):
     _, planes, count, cells = moved.shape
     chunks = cells // CHUNK
     fields = 2 * count
@@ -391,7 +391,6 @@
         second_kernel,
         grid=(chunks + 1,),
         in_specs=[
-            pl.BlockSpec(memory_space=pltpu.SMEM),
             pl.BlockSpec((planes, fields, CHUNK), lambda i: (0, 0, ahead(i))),
             rim_spec,
             rim_spec,
@@ -407,14 +406,55 @@
         ],
         cost_estimate=pl.CostEstimate(flops=10**8, transcendentals=0, bytes_accessed=10**7),
         name="second_partial",
-    )(flags, partial, below, above, moved, potential, table)
-
-
-def finish_kernel(partial, below, above, weights, out, density):
+    )(partial, below, above, moved, potential, table)
+
+
+BLOCK = 384
+LANES = 128
+EXACT = dict(precision=lax.Precision.HIGHEST, preferred_element_type=jnp.float32)
+
+
+def power_over(peak):
+    lift = 14.0 - jnp.floor(jnp.log2(jnp.where(peak > 0.0, peak, 1.0)))
+    return jnp.clip(lift, -110.0, 110.0)
+
+
+def packed(values, lift):
+    scaled = values * jnp.exp2(lift)
+    lane = lax.broadcasted_iota(jnp.int32, scaled.shape, 1)
+    coarse = scaled.astype(jnp.bfloat16).astype(jnp.float32)
+    rest = (scaled - coarse)[:, :1]
+    scaled = jnp.where(lane == 0, coarse, scaled)
+    scaled = jnp.where(lane == NZ, lift, scaled)
+    return jnp.where(lane == NZ + 1, rest, scaled)
+
+
+def unpacked(block):
+    lane = lax.broadcasted_iota(jnp.int32, block.shape, 1)
+    whole = jnp.where(lane == 0, block + block[:, NZ + 1 : NZ + 2], block)
+    return jnp.where(lane < NZ, whole * jnp.exp2(-block[:, NZ : NZ + 1]), 0.0)
+
+
+def spread_table(block, table):
+    table[...] = jnp.zeros(table.shape, table.dtype)
+    for part in range(BLOCK // NZ):
+        table[part * NZ : (part + 1) * NZ, part * LANES : (part + 1) * LANES] = block[...]
+
+
+def finish_kernel(shares, partial, below, above, z_block, y_table, out, chunks, z_table, rows, along_z, along_y, sent):
     planes = partial.shape[0]
-    count = out.shape[2]
+    fields = partial.shape[1]
+    count = fields // 2
+    groups = rows.shape[0]
+    members = chunks.shape[0]
+    step = pl.program_id(0)
+    per_step = CHUNK // BLOCK
     gain = 4.0 * bessel_terms[2] * 0.5 / energy_scale
-    weight = weights[:, :1]
+    field = lax.broadcasted_iota(jnp.int32, (fields, 1), 0) % count
+    weight = jnp.zeros((fields, 1), jnp.float32)
+    for at in range(count):
+        weight = jnp.where(field == at, shares[at], weight)
+    weight = weight * (1.0 / (count * lax.axis_size("band")))
     for plane in range(planes):
         value = partial[plane]
         if plane < REACH:
@@ -423,32 +463,164 @@
             value = value + gain * above[planes - 1 - plane].astype(jnp.float32)
         out[0, plane] = value[:count]
         out[1, plane] = value[count:]
-        density[plane : plane + 1, :] = jnp.sum(weight * (value * value), axis=0, keepdims=True)
-
-
-def finish(partial, below, above, weights):
+        total = jnp.sum(weight * (value * value), axis=0, keepdims=True)
+        for group in range(per_step):
+            rows[step * per_step + group, plane : plane + 1, :] = total[:, group * BLOCK : (group + 1) * BLOCK]
+
+    @pl.when(step == pl.num_programs(0) - 1)
+    def _():
+        padded = rows.shape[1]
+        spread_table(z_block, z_table)
+        turned = jnp.dot(rows[...].reshape(groups * padded, BLOCK), z_table[...], **EXACT)
+        for part in range(BLOCK // NZ):
+            along_z[part] = turned[:, part * LANES : (part + 1) * LANES]
+        for plane in range(planes):
+            for part in range(BLOCK // NZ):
+                along_y[part * groups : (part + 1) * groups, plane * LANES : (plane + 1) * LANES] = along_z[
+                    part, pl.ds(plane, groups, stride=padded), :
+                ]
+        waves = jnp.dot(y_table[...], along_y[...], **EXACT)
+        peak = jnp.max(jnp.max(jnp.abs(waves), axis=1, keepdims=True), axis=0, keepdims=True)
+        lift = power_over(peak)
+        for part in range(chunks.shape[3] // LANES):
+            for plane in range(planes):
+                block = waves[part * members : (part + 1) * members, plane * LANES : (plane + 1) * LANES]
+                sent[part, pl.ds(plane, members, stride=planes), :] = packed(block, lift)
+        for member in range(members):
+            for quarter in range(planes // 4):
+                start = member * planes + quarter * 4
+                for part in range(chunks.shape[3] // LANES):
+                    lanes = slice(part * LANES, (part + 1) * LANES)
+                    chunks[member, quarter, :, lanes] = sent[part, start : start + 4, :]
+
+
+def finish(partial, below, above, occupations, z_table, y_table, members):
     planes, fields, cells = partial.shape
-    chunks = cells // CHUNK
     rim_spec = pl.BlockSpec((REACH, fields, CHUNK), lambda i: (0, 0, i))
+    groups = cells // BLOCK
+    padded = -(-planes // 8) * 8
+    width = NY // members * LANES
+    whole = lambda shape: pl.BlockSpec(shape, lambda i: (0,) * len(shape))
+    wave_shape = (members, planes // 4, 4, width)
     return pl.pallas_call(
         finish_kernel,
-        grid=(chunks,),
+        grid=(cells // CHUNK,),
         in_specs=[
+            pl.BlockSpec(memory_space=pltpu.SMEM),
             pl.BlockSpec((planes, fields, CHUNK), lambda i: (0, 0, i)),
             rim_spec,
             rim_spec,
-            pl.BlockSpec((fields, 128), lambda i: (0, 0)),
-        ],
-        out_specs=[
-            pl.BlockSpec((2, planes, fields // 2, CHUNK), lambda i: (0, 0, 0, i)),
-            pl.BlockSpec((planes, CHUNK), lambda i: (0, i)),
-        ],
+            whole(z_table.shape),
+            whole(y_table.shape),
+        ],
+        out_specs=[pl.BlockSpec((2, planes, fields // 2, CHUNK), lambda i: (0, 0, 0, i)), whole(wave_shape)],
         out_shape=[
             jax.ShapeDtypeStruct((2, planes, fields // 2, cells), jnp.float32),
-            jax.ShapeDtypeStruct((planes, cells), jnp.float32),
+            jax.ShapeDtypeStruct(wave_shape, jnp.float32),
+        ],
+        scratch_shapes=[
+            pltpu.VMEM((BLOCK, BLOCK // NZ * LANES), jnp.float32),
+            pltpu.VMEM((groups, padded, BLOCK), jnp.float32),
+            pltpu.VMEM((BLOCK // NZ, groups * padded, LANES), jnp.float32),
+            pltpu.VMEM((NY, planes * LANES), jnp.float32),
+            pltpu.VMEM((width // LANES, members * planes, LANES), jnp.float32),
         ],
         name="finish",
-    )(partial, below, above, weights)
+    )(occupations, partial, below, above, z_table, y_table)
+
+
+def column_kernel(arrived, multiplier, x_table, back_table, chunks, raw, columns, both):
+    members, quarters, _, width = arrived.shape
+    planes = quarters * 4
+    blocks = chunks.shape[0]
+    length = blocks * planes
+    for member in range(members):
+        for quarter in range(quarters):
+            start = member * planes + quarter * 4
+            raw[start : start + 4, :] = arrived[member, quarter]
+    for part in range(width // LANES):
+        lanes = slice(part * LANES, (part + 1) * LANES)
+        total = unpacked(raw[:length, lanes])
+        for band in range(1, members // blocks):
+            total = total + unpacked(raw[band * length : (band + 1) * length, lanes])
+        columns[:, lanes] = total
+    waves = jnp.dot(x_table[...], columns[...], **EXACT) * multiplier[...]
+    field = jnp.dot(back_table[...], waves, **EXACT)
+    for index, values in enumerate((columns[...], field)):
+        peak = jnp.max(jnp.max(jnp.abs(values), axis=1, keepdims=True), axis=0, keepdims=True)
+        lift = power_over(peak)
+        for part in range(width // LANES):
+            at = index * width + part * LANES
+            both[:, at : at + LANES] = packed(values[:, part * LANES : (part + 1) * LANES], lift)
+    for block in range(blocks):
+        for quarter in range(quarters):
+            start = block * planes + quarter * 4
+            chunks[block, quarter] = both[start : start + 4, :]
+
+
+def column_waves(arrived, multiplier, x_table, blocks):
+    members, quarters, _, width = arrived.shape
+    length = x_table.shape[0]
+    return pl.pallas_call(
+        column_kernel,
+        out_shape=jax.ShapeDtypeStruct((blocks, quarters, 4, 2 * width), jnp.float32),
+        scratch_shapes=[
+            pltpu.VMEM((members * quarters * 4, width), jnp.float32),
+            pltpu.VMEM((length, width), jnp.float32),
+            pltpu.VMEM((length, 2 * width), jnp.float32),
+        ],
+        name="column_waves",
+    )(arrived, multiplier, jnp.asarray(x_table), jnp.asarray(x_table.T))
+
+
+def return_kernel(arrived, y_back, z_block, density, hartree, z_table, raw, along_y, along_z, result):
+    members, quarters, _, width = arrived.shape
+    width //= 2
+    planes = quarters * 4
+    groups = result.shape[1] // planes
+    spread_table(z_block, z_table)
+    for member in range(members):
+        for quarter in range(quarters):
+            start = member * planes + quarter * 4
+            for part in range(2 * width // LANES):
+                raw[part, start : start + 4, :] = arrived[member, quarter, :, part * LANES : (part + 1) * LANES]
+    for index, out in enumerate((density, hartree)):
+        for plane in range(planes):
+            for part in range(width // LANES):
+                block = raw[index * (width // LANES) + part, pl.ds(plane, members, stride=planes), :]
+                along_y[part * members : (part + 1) * members, plane * LANES : (plane + 1) * LANES] = unpacked(block)
+        waves = jnp.dot(y_back[...], along_y[...], **EXACT)
+        for plane in range(planes):
+            for part in range(BLOCK // NZ):
+                along_z[plane * groups : (plane + 1) * groups, part * LANES : (part + 1) * LANES] = waves[
+                    part * groups : (part + 1) * groups, plane * LANES : (plane + 1) * LANES
+                ]
+        cells = lax.dot_general(along_z[...], z_table[...], (((1,), (1,)), ((), ())), **EXACT)
+        for tile in range(BLOCK // LANES):
+            result[tile] = cells[:, tile * LANES : (tile + 1) * LANES]
+        for group in range(groups):
+            for tile in range(BLOCK // LANES):
+                at = group * BLOCK + tile * LANES
+                out[:, at : at + LANES] = result[tile, pl.ds(group, planes, stride=groups), :]
+
+
+def return_waves(arrived, y_table, z_table, cells):
+    members, quarters, _, width = arrived.shape
+    planes = quarters * 4
+    groups = cells // BLOCK
+    plane_shape = jax.ShapeDtypeStruct((planes, cells), jnp.float32)
+    return pl.pallas_call(
+        return_kernel,
+        out_shape=[plane_shape, plane_shape],
+        scratch_shapes=[
+            pltpu.VMEM((BLOCK, BLOCK // NZ * LANES), jnp.float32),
+            pltpu.VMEM((width // LANES, members * planes, LANES), jnp.float32),
+            pltpu.VMEM((NY, planes * LANES), jnp.float32),
+            pltpu.VMEM((planes * groups, BLOCK // NZ * LANES), jnp.float32),
+            pltpu.VMEM((BLOCK // LANES, planes * groups, LANES), jnp.float32),
+        ],
+        name="return_waves",
+    )(arrived, y_table, z_table)
 
 
 def wave_basis(length):
@@ -465,83 +637,64 @@
     return np.asarray(rows, np.float32), (2.0 * math.pi / length * np.asarray(waves, np.float64)) ** 2
 
 
-def hartree_waves(partial_density):
-    planes = partial_density.shape[0]
+def wave_tables(members, length):
+    z_basis, z_squares = wave_basis(NZ)
+    y_basis, y_squares = wave_basis(NY)
+    x_basis, x_squares = wave_basis(length)
+    parts = BLOCK // NZ
+    z_table = np.pad(z_basis.T, ((0, 0), (0, LANES - NZ)))
+    rows = NY // members
+    y_table = y_basis.reshape(members, rows, NY // parts, parts).transpose(1, 0, 3, 2).reshape(NY, NY)
+    return z_table, y_table, x_basis, (x_squares, y_squares, z_squares)
+
+
+def density_and_field(waves, tables, cells):
     bands = lax.axis_size("band")
     blocks = lax.axis_size("space")
-    whole = ("band", "space")
-    exact = dict(precision=lax.Precision.HIGHEST, preferred_element_type=jnp.float32)
-    z_basis, z_squares = wave_basis(NZ)
-    y_basis, y_squares = wave_basis(NY)
-    x_basis, x_squares = wave_basis(planes * blocks)
-    grid = partial_density.reshape(planes, NY, NZ)
-    spectral = jnp.einsum("xyz,cz->xyc", grid, z_basis, **exact)
-    spectral = jnp.einsum("by,xyc->xbc", y_basis, spectral, **exact)
-    columns = lax.all_to_all(spectral, whole, split_axis=1, concat_axis=0, tiled=True)
-    rows = columns.shape[1]
-    columns = jnp.sum(columns.reshape(bands, planes * blocks, rows, NZ), axis=0)
+    members, quarters, _, width = waves.shape
+    z_table, y_table, x_table, (x_squares, y_squares, z_squares) = tables
+    exchange = lambda chunks: lax.all_to_all(
+        chunks.astype(jnp.float16), ("band", "space"), split_axis=0, concat_axis=0, tiled=True
+    ).astype(jnp.float32)
+    rows = NY // members
     place = (lax.axis_index("band") * blocks + lax.axis_index("space")) * rows
     squares = (
         jnp.asarray(x_squares, jnp.float32)[:, None, None]
         + lax.dynamic_slice_in_dim(jnp.asarray(y_squares, jnp.float32), place, rows)[None, :, None]
-        + jnp.asarray(z_squares, jnp.float32)[None, None, :]
-    )
-    kernel = jnp.where(squares > 0, 4.0 * math.pi / jnp.where(squares > 0, squares, 1.0), 0.0)
-    columns = jnp.einsum("ax,xbc->abc", x_basis, columns, **exact) * kernel
-    columns = jnp.einsum("ax,abc->xbc", x_basis, columns, **exact)
-    spread = jnp.broadcast_to(columns[None], (bands, *columns.shape)).reshape(-1, rows, NZ)
-    spectral = lax.all_to_all(spread, whole, split_axis=0, concat_axis=1, tiled=True)
-    spectral = jnp.einsum("by,xbc->xyc", y_basis, spectral, **exact)
-    field = jnp.einsum("cz,xyc->xyz", z_basis, spectral, **exact)
-    return field.reshape(planes, NY * NZ)
-
-
-def ring_shift(x, axis, by):
-    count = lax.axis_size(axis)
-    return lax.ppermute(x, axis, [(i, (i + by) % count) for i in range(count)])
-
-
-def band_sum(partial):
-    bands = lax.axis_size("band")
-    mine = lax.axis_index("band")
-    width = partial.shape[1] // bands
-    piece = lambda shift: lax.dynamic_slice_in_dim(partial, (mine + shift) % bands * width, width, 1)
-    own = piece(0)
-    for shift in range(1, bands):
-        own = own + ring_shift(piece(shift), "band", shift)
-    total = jnp.zeros_like(partial)
-    total = lax.dynamic_update_slice_in_dim(total, own, mine * width, 1)
-    for shift in range(1, bands):
-        arrived = ring_shift(own, "band", shift)
-        total = lax.dynamic_update_slice_in_dim(total, arrived, (mine - shift) % bands * width, 1)
-    return total
+        + jnp.asarray(np.pad(z_squares, (0, LANES - NZ)), jnp.float32)[None, None, :]
+    )
+    used = lax.broadcasted_iota(jnp.int32, squares.shape, 2) < NZ
+    multiplier = jnp.where(
+        (squares > 0) & used, 4.0 * math.pi / jnp.where(squares > 0, squares, 1.0), 0.0
+    ).reshape(-1, width)
+    both = column_waves(exchange(waves), multiplier, x_table, blocks)
+    spread = jnp.broadcast_to(both.astype(jnp.float16)[None], (bands, *both.shape)).reshape(members, *both.shape[1:])
+    return return_waves(exchange(spread), jnp.asarray(y_table.T), jnp.asarray(z_table), cells)
 
 
 def per_device_blocks(orbitals, potential, occupations):
-    count = orbitals.shape[1]
     moved = orbitals.transpose(0, 2, 1, 3)
     table = plane_table()
-    place = lax.axis_index("space")
-    flags = jnp.stack([place > 0, place < lax.axis_size("space") - 1]).astype(jnp.float32)
     lower, upper = rim_copies(moved)
     below = from_behind(upper, "space", 1)
     above = from_behind(lower, "space", -1)
     partial, to_lower, to_upper = first_partial(moved, potential, table)
     terms_below = from_behind(to_upper, "space", 1)
     terms_above = from_behind(to_lower, "space", -1)
-    partial = second_partial(flags, partial, below, above, moved, potential, table)
-    weights = occupations / (count * lax.axis_size("band"))
-    weights = jnp.broadcast_to(jnp.concatenate([weights, weights])[:, None], (2 * count, 128))
-    propagated, partial_density = finish(partial, terms_below, terms_above, weights)
-    hartree = hartree_waves(partial_density)
-    density = band_sum(partial_density)
+    partial = second_partial(partial, below, above, moved, potential, table)
+    members = lax.axis_size("band") * lax.axis_size("space")
+    tables = wave_tables(members, orbitals.shape[2] * lax.axis_size("space"))
+    propagated, waves = finish(
+        partial, terms_below, terms_above, occupations, jnp.asarray(tables[0]), jnp.asarray(tables[1]), members
+    )
+    density, hartree = density_and_field(waves, tables, orbitals.shape[3])
     return (propagated.transpose(0, 2, 1, 3), density, hartree)
 
 
 def per_device(orbitals, potential, occupations):
     _, count, planes, cells = orbitals.shape
     columns = NY % (lax.axis_size("space") * lax.axis_size("band"))
-    if planes < 2 * REACH or count != 4 or cells % CHUNK or CHUNK % NZ or MARGIN != REACH * NZ or columns:
+    if planes < 2 * REACH or planes % 4 or count != 4 or cells % CHUNK or PERIOD % NZ or MARGIN != REACH * NZ or columns:
         return per_device_general(orbitals, potential, occupations)
     return per_device_blocks(orbitals, potential, occupations)
 

time: 133 us -> 96.8 us (0.73)
  waiting for transfers between devices: 40.9 us -> 10.4 us
  blocking collectives: 0 us -> 18.9 us
  starting transfers between devices: 33.5 us -> 19.3 us
  local copies, waits for them, and re-layouts: 9.51 us -> 3.03 us
  matrix products: 4.83 us -> 0 us
  other arithmetic: 1.8 us -> 5.84 us
  Pallas kernels: 39.8 us -> 37.8 us
    all_to_all x2 -> x1, waiting for transfers between devices: 40.6 us -> 10.4 us  [density_and_field(): lax.all_to_all(chunks.astype(jnp.float16), ('band', 'space'), split_axis=...]
    all_to_all x0 -> x1, blocking collectives: none -> 18.9 us  [density_and_field(): lax.all_to_all(chunks.astype(jnp.float16), ('band', 'space'), split_axis=...]
    ppermute x6 -> x0, starting transfers between devices: 10.7 us -> none  [ring_shift(): return lax.ppermute(x, axis, [(i, (i + by) % count) for i in range(count)])]
    pallas_call x2 -> x4, Pallas kernels: 14.8 us -> 19.9 us  [the longest x1 8.63 us: finish(): pl.pallas_call(finish_kernel, grid=(cells // CHUNK,), in_specs=[pl.BlockS...]
    dot_general x6 -> x0, matrix products: 4.83 us -> none  [the longest x1 1.42 us: hartree_waves(): spectral = jnp.einsum('xyz,cz->xyc', grid, z_basis, **exact)]
    convert_element_type x1 -> x4, other arithmetic: 0.65 us -> 5.05 us  [the longest x2 2.15 us: density_and_field(): exchange = lambda chunks: lax.all_to_all(chunks.astype(jnp.float16), ('ba...]
    pallas_call x1, Pallas kernels: 11.9 us -> 8.16 us  [first_partial(): pl.pallas_call(first_kernel, grid=(chunks,), in_specs=[pl.BlockSpec((2, p...]
    all_to_all x2 -> x1, starting transfers between devices: 12.7 us -> 9.18 us  [density_and_field(): lax.all_to_all(chunks.astype(jnp.float16), ('band', 'space'), split_axis=...]
  transfers between devices with their start and end apart: 12 -> 5, of which waited for: 3 -> 1; matrix products, arithmetic and copies ran while one was open for 6% -> 1% of each run, Pallas kernels for 19% -> 19%
where the time goes in v1:
time: 96.8 us; the launch traced here: 96.1 us
  Pallas kernels  37.8 us (39%)
  starting transfers between devices  19.3 us (20%)
  blocking collectives  18.9 us (20%)
  waiting for transfers between devices  10.4 us (11%)
  other arithmetic  5.84 us (6%)
  local copies, waits for them, and re-layouts  3.03 us (3%)
    all_to_all x1, blocking collectives, density_and_field(): lax.all_to_all(chunks.astype(jnp.float16), ('band', 'space'), split_axis=...  18.9 us
    all_to_all x1, waiting for transfers between devices, density_and_field(): lax.all_to_all(chunks.astype(jnp.float16), ('band', 'space'), split_axis=...  10.4 us
    ppermute x4, starting transfers between devices, from_behind(): return lax.ppermute(x, axis, pairs)  10.1 us
    pallas_call x1, Pallas kernels, second_partial(): pl.pallas_call(second_kernel, grid=(chunks + 1,), in_specs=[pl.BlockSpec(...  9.78 us
    all_to_all x1, starting transfers between devices, density_and_field(): lax.all_to_all(chunks.astype(jnp.float16), ('band', 'space'), split_axis=...  9.18 us
    pallas_call x1, Pallas kernels, finish(): pl.pallas_call(finish_kernel, grid=(cells // CHUNK,), in_specs=[pl.BlockS...  8.63 us
    pallas_call x1, Pallas kernels, first_partial(): pl.pallas_call(first_kernel, grid=(chunks,), in_specs=[pl.BlockSpec((2, p...  8.16 us
    pallas_call x1, Pallas kernels, return_waves(): pl.pallas_call(return_kernel, out_shape=[plane_shape, plane_shape], scrat...  5.55 us
  transfers between devices with their start and end apart: 5, of which 1 were waited for; matrix products, arithmetic and copies ran while one was open for 1% of the time, Pallas kernels for 19%

profile of v1, /device:TPU:0, one launch (start us, length us, event | category | flops | bytes accessed | tf_op | source)
XLA Modules:
  0.0 96.1 jit_solution(4779984930397034689)
XLA Ops:
  0.6 2.7 %rim_copies.1 = (bf16[4,8,9216]{2,1,0:T(8,128)(2,1)}, bf16[4,8,9216]{2,1,0:T(8,128)(2,1)}) custom-call(f32[2,12,4,9216]{3,2,1,0:T(4,128)} %bitcast.12), custom_call_target="tpu_custom_call" | custom-call | tf_op jit(solution)/shard_map/rim_copies/pallas_call | solution.py:210
  3.3 2.4 %collective-permute-start = (bf16[4,8,9216]{2,1,0:T(8,128)(2,1)}, bf16[4,8,9216]{2,1,0:T(8,128)(2,1)S(1)}, u32[]{:S(2)}, u32[]{:S(2)}) collective-permute-start(bf16[4,8,9216]{2,1,0:T(8,128)(2,1)} %get-tuple-element.13), channel_id=1, source_target_pairs={{0,1},{1,2},{2,3},{3,4},{4,5},{5,6},{6,7},{8,9},{9,10},{10,11},{11... | collective-permute-start | bytes 1769480 | tf_op jit(solution)/shard_map/ppermute | solution.py:25
  5.8 0.0 copy-start.4
  5.8 0.0 copy-start.5
  5.8 1.3 %collective-permute-start.1 = (bf16[4,8,9216]{2,1,0:T(8,128)(2,1)}, bf16[4,8,9216]{2,1,0:T(8,128)(2,1)S(1)}, u32[]{:S(2)}, u32[]{:S(2)}) collective-permute-start(bf16[4,8,9216]{2,1,0:T(8,128)(2,1)} %get-tuple-element.14), channel_id=1, source_target_pairs={{1,0},{2,1},{3,2},{4,3},{5,4},{6,5},{7,6},{9,8},{10,9},{11,10},{12... | collective-permute-start | bytes 1769480 | tf_op jit(solution)/shard_map/ppermute | solution.py:25
  7.1 8.2 %first_partial.1 = (f32[12,8,9216]{2,1,0:T(8,128)}, bf16[4,8,9216]{2,1,0:T(8,128)(2,1)}, bf16[4,8,9216]{2,1,0:T(8,128)(2,1)}) custom-call(f32[2,12,4,9216]{3,2,1,0:T(4,128)} %bitcast.13, f32[2,12,4,9216]{3,2,1,0:T(4,128)} %bitcast.14, f32[2,12,4,9216]{3,2,1,0:T(4,128)} %bitcast.15, f32[12,9216]{1,0:T(8,128)} %potential.3, ...), custom_call_target="tpu_custom_call" | custom-call | flops 100000000 | bytes 10000000 | tf_op jit(solution)/shard_map/first_partial/pallas_call | solution.py:284
  15.2 5.1 %collective-permute-start.2 = (bf16[4,8,9216]{2,1,0:T(8,128)(2,1)}, bf16[4,8,9216]{2,1,0:T(8,128)(2,1)S(1)}, u32[]{:S(2)}, u32[]{:S(2)}) collective-permute-start(bf16[4,8,9216]{2,1,0:T(8,128)(2,1)} %get-tuple-element.15), channel_id=1, source_target_pairs={{0,1},{1,2},{2,3},{3,4},{4,5},{5,6},{6,7},{8,9},{9,10},{10,11},{11... | collective-permute-start | bytes 1769480 | tf_op jit(solution)/shard_map/ppermute | solution.py:25
  20.4 1.3 %collective-permute-start.3 = (bf16[4,8,9216]{2,1,0:T(8,128)(2,1)}, bf16[4,8,9216]{2,1,0:T(8,128)(2,1)S(1)}, u32[]{:S(2)}, u32[]{:S(2)}) collective-permute-start(bf16[4,8,9216]{2,1,0:T(8,128)(2,1)} %get-tuple-element.16), channel_id=1, source_target_pairs={{1,0},{2,1},{3,2},{4,3},{5,4},{6,5},{7,6},{9,8},{10,9},{11,10},{12... | collective-permute-start | bytes 1769480 | tf_op jit(solution)/shard_map/ppermute | solution.py:25
  21.7 0.0 copy-done.4
  21.7 0.1 dynamic_slice.3
  21.8 0.0 copy-done.5
  21.8 0.0 collective-permute-done.below
  21.8 0.0 copy-start.2
  21.8 0.0 collective-permute-done.1.above
  21.8 0.0 copy-start.3
  21.8 0.8 copy-done.2
  22.6 0.2 copy-done.3
  22.8 9.8 %second_partial.1.partial = f32[12,8,9216]{2,1,0:T(8,128)} custom-call(f32[12,8,9216]{2,1,0:T(8,128)} %get-tuple-element.12.partial, bf16[4,8,9216]{2,1,0:T(8,128)(2,1)} %copy-done.2, bf16[4,8,9216]{2,1,0:T(8,128)(2,1)} %copy-done.3, f32[2,12,4,9216]{3,2,1,0:T(4,128)} %bitcast.16, f32[12,9216]{1,0:T(8,128)} %potential.3, ...), custom_call_target="tpu_custom_call" | custom-call | flops 100000000 | bytes 10000000 | tf_op jit(solution)/shard_map/second_partial/pallas_call | solution.py:390
  32.6 0.0 collective-permute-done.2.below
  32.6 0.0 copy-start
  32.6 0.0 collective-permute-done.3.above
  32.6 0.8 copy-done
  33.4 0.0 copy-start.1
  33.4 0.8 copy-done.1
  34.2 8.6 %finish.1 = (f32[2,12,4,9216]{3,2,1,0:T(4,128)}, f32[32,3,4,384]{3,2,1,0:T(4,128)}) custom-call(f32[4]{0:T(128)} %shares.1, f32[12,8,9216]{2,1,0:T(8,128)} %second_partial.1.partial, bf16[4,8,9216]{2,1,0:T(8,128)(2,1)} %copy-done, bf16[4,8,9216]{2,1,0:T(8,128)(2,1)} %copy-done.1, f32[96,128]{1,0:T(8,128)} %constant.41.clone.z_block, ...), custom_call_target="tpu_custom_call" | custom-call | tf_op jit(solution)/shard_map/finish/pallas_call | solution.py:505
  42.9 1.9 %convert_element_type.12 = f16[32,3,4,384]{3,2,1,0:T(4,128)(2,1)} convert(f32[32,3,4,384]{3,2,1,0:T(4,128)} %get-tuple-element.18) | non-fusion elementwise | flops 147456 | bytes 884736 | tf_op jit(solution)/shard_map/convert_element_type | solution.py:657
  44.7 9.2 %all-to-all-start = ((f16[32,3,4,384]{3,2,1,0:T(4,128)(2,1)}), f16[32,3,4,384]{3,2,1,0:T(4,128)(2,1)S(1)}, u32[]{:S(2)}, u32[]{:S(2)}) async-start(f16[32,3,4,384]{3,2,1,0:T(4,128)(2,1)} %convert_element_type.12), calls=%async_computation | async-start | bytes 589824 | tf_op jit(solution)/shard_map/all_to_all | solution.py:656
  53.9 0.1 broadcast_add_fusion
  54.0 0.2 add.49
  54.2 0.7 fusion.1.multiplier
  54.9 10.4 %all-to-all-done = f16[32,3,4,384]{3,2,1,0:T(4,128)(2,1)S(1)} async-done(((f16[32,3,4,384]{3,2,1,0:T(4,128)(2,1)}), f16[32,3,4,384]{3,2,1,0:T(4,128)(2,1)S(1)}, u32[]{:S(2)}, u32[]{:S(2)}) %all-to-all-start) | async-done | bytes 294944 | tf_op jit(solution)/shard_map/all_to_all | solution.py:656
  65.3 0.9 convert_element_type.13.arrived
  66.2 3.0 %column_waves.1 = f32[8,3,4,768]{3,2,1,0:T(4,128)} custom-call(f32[32,3,4,384]{3,2,1,0:T(4,128)} %convert_element_type.13.arrived, f32[96,384]{1,0:T(8,128)} %fusion.1.multiplier, f32[96,96]{1,0:T(8,128)} %constant.45.clone.x_table, f32[96,96]{1,0:T(8,128)} %constant.46.clone.back_table), custom_call_target="tpu_custom_call" | custom-call | tf_op jit(solution)/shard_map/column_waves/pallas_call | solution.py:564
  69.2 1.0 %convert_element_type.14 = f16[8,3,4,768]{3,2,1,0:T(4,128)(2,1)S(1)} convert(f32[8,3,4,768]{3,2,1,0:T(4,128)} %column_waves.1) | non-fusion elementwise | flops 73728 | bytes 442368 | tf_op jit(solution)/shard_map/convert_element_type | solution.py:671
  70.3 0.2 broadcast_in_dim.8
  70.4 18.9 %all_to_all.10 = f16[32,3,4,768]{3,2,1,0:T(4,128)(2,1)S(1)} all-to-all(f16[32,3,4,768]{3,2,1,0:T(4,128)(2,1)S(1)} %bitcast.17), channel_id=1, replica_groups=mesh['band'=4,'space'=8] {'band','space'}, dimensions={0} | all-to-all | bytes 1179648 | tf_op jit(solution)/shard_map/all_to_all | solution.py:656
  89.3 1.2 %convert_element_type.15.arrived = f32[32,3,4,768]{3,2,1,0:T(4,128)} convert(f16[32,3,4,768]{3,2,1,0:T(4,128)(2,1)S(1)} %all_to_all.10) | non-fusion elementwise | flops 294912 | bytes 1769472 | tf_op jit(solution)/shard_map/convert_element_type | solution.py:658
  90.5 5.6 %return_waves.1 = (f32[12,9216]{1,0:T(8,128)}, f32[12,9216]{1,0:T(8,128)}) custom-call(f32[32,3,4,768]{3,2,1,0:T(4,128)} %convert_element_type.15.arrived, f32[96,96]{1,0:T(8,128)} %constant.47.clone.y_back, f32[96,128]{1,0:T(8,128)} %constant.41.clone.z_block), custom_call_target="tpu_custom_call" | custom-call | tf_op jit(solution)/shard_map/return_waves/pallas_call | solution.py:612
  (3 shorter events, 0.0 us)
Async XLA Ops:
  3.3 18.5 %collective-permute-start = (bf16[4,8,9216]{2,1,0:T(8,128)(2,1)}, bf16[4,8,9216]{2,1,0:T(8,128)(2,1)S(1)}, u32[]{:S(2)}, u32[]{:S(2)}) collective-permute-start(bf16[4,8,9216]{2,1,0:T(8,128)(2,1)} %get-tuple-element.13), channel_id=1, source_target_pairs={{0,1},{1,2},{2,3},{3,4},{4,5},{5,6},{6,7},{8,9},{9,10},{10,11},{11... | collective-permute-start | bytes 1769480 | tf_op jit(solution)/shard_map/ppermute | solution.py:25
  5.8 15.9 %copy-start.4 = (f32[96]{0:T(128)S(1)}, f32[96]{0:T(128)}, u32[]{:S(2)}) copy-start(f32[96]{0:T(128)} %constant.43.clone) | copy-start | bytes 1156
  5.8 16.0 %copy-start.5 = (f32[128]{0:T(128)S(1)}, f32[128]{0:T(128)}, u32[]{:S(2)}) copy-start(f32[128]{0:T(128)} %constant.44.clone) | copy-start | bytes 1540
  5.8 16.0 %collective-permute-start.1 = (bf16[4,8,9216]{2,1,0:T(8,128)(2,1)}, bf16[4,8,9216]{2,1,0:T(8,128)(2,1)S(1)}, u32[]{:S(2)}, u32[]{:S(2)}) collective-permute-start(bf16[4,8,9216]{2,1,0:T(8,128)(2,1)} %get-tuple-element.14), channel_id=1, source_target_pairs={{1,0},{2,1},{3,2},{4,3},{5,4},{6,5},{7,6},{9,8},{10,9},{11,10},{12... | collective-permute-start | bytes 1769480 | tf_op jit(solution)/shard_map/ppermute | solution.py:25
  15.2 17.4 %collective-permute-start.2 = (bf16[4,8,9216]{2,1,0:T(8,128)(2,1)}, bf16[4,8,9216]{2,1,0:T(8,128)(2,1)S(1)}, u32[]{:S(2)}, u32[]{:S(2)}) collective-permute-start(bf16[4,8,9216]{2,1,0:T(8,128)(2,1)} %get-tuple-element.15), channel_id=1, source_target_pairs={{0,1},{1,2},{2,3},{3,4},{4,5},{5,6},{6,7},{8,9},{9,10},{10,11},{11... | collective-permute-start | bytes 1769480 | tf_op jit(solution)/shard_map/ppermute | solution.py:25
  20.4 12.2 %collective-permute-start.3 = (bf16[4,8,9216]{2,1,0:T(8,128)(2,1)}, bf16[4,8,9216]{2,1,0:T(8,128)(2,1)S(1)}, u32[]{:S(2)}, u32[]{:S(2)}) collective-permute-start(bf16[4,8,9216]{2,1,0:T(8,128)(2,1)} %get-tuple-element.16), channel_id=1, source_target_pairs={{1,0},{2,1},{3,2},{4,3},{5,4},{6,5},{7,6},{9,8},{10,9},{11,10},{12... | collective-permute-start | bytes 1769480 | tf_op jit(solution)/shard_map/ppermute | solution.py:25
  21.8 0.8 copy-start.2
  21.8 1.0 %copy-start.3 = (bf16[4,8,9216]{2,1,0:T(8,128)(2,1)}, bf16[4,8,9216]{2,1,0:T(8,128)(2,1)S(1)}, u32[]{:S(2)}) copy-start(bf16[4,8,9216]{2,1,0:T(8,128)(2,1)S(1)} %collective-permute-done.1.above) | copy-start | bytes 1769476
  32.6 0.8 copy-start
  33.4 0.8 copy-start.1
  44.7 20.6 %all-to-all-start = ((f16[32,3,4,384]{3,2,1,0:T(4,128)(2,1)}), f16[32,3,4,384]{3,2,1,0:T(4,128)(2,1)S(1)}, u32[]{:S(2)}, u32[]{:S(2)}) async-start(f16[32,3,4,384]{3,2,1,0:T(4,128)(2,1)} %convert_element_type.12), calls=%async_computation | async-start | bytes 589824 | tf_op jit(solution)/shard_map/all_to_all | solution.py:656

commit v2 on v1

--- a/solution.py
+++ b/solution.py
@@ -164,6 +164,7 @@
 TABLE_SCALE = 5040.0
 PERIOD = 768
 CHUNK = 2304
+WIDE_CHUNK = 4608
 WINDOW = 1024
 TILE = 256
 MARGIN = 384
@@ -206,7 +207,7 @@
 
 def rim_copies(moved):
     _, planes, count, cells = moved.shape
-    rim = jax.ShapeDtypeStruct((REACH, 2 * count, cells), jnp.bfloat16)
+    rim = pltpu.VMEM((REACH, 2 * count, cells), jnp.bfloat16)
     return pl.pallas_call(
         rim_kernel,
         in_specs=[pl.BlockSpec(memory_space=pl.ANY)],
@@ -271,7 +272,7 @@
                 for offset in range(plane + 1, REACH + 1):
                     term = stencil_coeffs[offset] * order[offset - plane - 1]
                     total = term if total is None else total + term
-                rim[plane, :, lanes] = total.astype(jnp.bfloat16)
+                rim[plane, :, pl.ds(pl.multiple_of(step * CHUNK + phase * TILE, TILE), TILE)] = total.astype(jnp.bfloat16)
 
 
 def first_partial(moved, potential, table):
@@ -279,8 +280,8 @@
     chunks = cells // CHUNK
     margins = CHUNK // MARGIN
     fields = 2 * count
-    rim = jax.ShapeDtypeStruct((REACH, fields, cells), jnp.bfloat16)
-    rim_spec = pl.BlockSpec((REACH, fields, CHUNK), lambda i: (0, 0, i))
+    rim = pltpu.VMEM((REACH, fields, cells), jnp.bfloat16)
+    rim_spec = pl.BlockSpec(memory_space=pltpu.VMEM)
     return pl.pallas_call(
         first_kernel,
         grid=(chunks,),
@@ -339,9 +340,9 @@
             first = partial[plane]
             for offset in range(1, REACH + 1):
                 if plane - offset < 0:
-                    first = first - half_scale * stencil_coeffs[offset] * below[REACH + plane - offset].astype(jnp.float32)
+                    first = first - half_scale * stencil_coeffs[offset] * below[REACH + plane - offset, :, pl.ds(base, CHUNK)].astype(jnp.float32)
                 if plane + offset >= planes:
-                    first = first - half_scale * stencil_coeffs[offset] * above[plane + offset - planes].astype(jnp.float32)
+                    first = first - half_scale * stencil_coeffs[offset] * above[plane + offset - planes, :, pl.ds(base, CHUNK)].astype(jnp.float32)
             firsts[rows, pl.ds(base, CHUNK)] = first
             copies[rows, pl.ds(pl.multiple_of(base + MARGIN, 128), CHUNK)] = first.astype(jnp.bfloat16)
 
@@ -386,7 +387,7 @@
     fields = 2 * count
     ahead = lambda i: jnp.minimum(i, chunks - 1)
     behind = lambda i: jnp.maximum(i - 1, 0)
-    rim_spec = pl.BlockSpec((REACH, fields, CHUNK), lambda i: (0, 0, ahead(i)))
+    rim_spec = pl.BlockSpec(memory_space=pltpu.VMEM)
     return pl.pallas_call(
         second_kernel,
         grid=(chunks + 1,),
@@ -411,7 +412,23 @@
 
 BLOCK = 384
 LANES = 128
-EXACT = dict(precision=lax.Precision.HIGHEST, preferred_element_type=jnp.float32)
+
+
+def halves(values):
+    coarse = values.astype(jnp.bfloat16)
+    return coarse, (values - coarse.astype(jnp.float32)).astype(jnp.bfloat16)
+
+
+def exact_product(left, right):
+    return jnp.dot(left, right, precision=lax.Precision.HIGHEST, preferred_element_type=jnp.float32)
+
+
+def product(left, right, contract=0):
+    numbers = (((1,), (contract,)), ((), ()))
+    dot = lambda a, b: lax.dot_general(a, b, numbers, preferred_element_type=jnp.float32)
+    left_coarse, left_rest = halves(left)
+    right_coarse, right_rest = halves(right)
+    return dot(left_coarse, right_coarse) + (dot(left_coarse, right_rest) + dot(left_rest, right_coarse))
 
 
 def power_over(peak):
@@ -448,7 +465,8 @@
     groups = rows.shape[0]
     members = chunks.shape[0]
     step = pl.program_id(0)
-    per_step = CHUNK // BLOCK
+    per_step = WIDE_CHUNK // BLOCK
+    lanes = pl.ds(pl.multiple_of(step * WIDE_CHUNK, LANES), WIDE_CHUNK)
     gain = 4.0 * bessel_terms[2] * 0.5 / energy_scale
     field = lax.broadcasted_iota(jnp.int32, (fields, 1), 0) % count
     weight = jnp.zeros((fields, 1), jnp.float32)
@@ -458,9 +476,9 @@
     for plane in range(planes):
         value = partial[plane]
         if plane < REACH:
-            value = value + gain * below[plane].astype(jnp.float32)
+            value = value + gain * below[plane, :, lanes].astype(jnp.float32)
         if planes - 1 - plane < REACH:
-            value = value + gain * above[planes - 1 - plane].astype(jnp.float32)
+            value = value + gain * above[planes - 1 - plane, :, lanes].astype(jnp.float32)
         out[0, plane] = value[:count]
         out[1, plane] = value[count:]
         total = jnp.sum(weight * (value * value), axis=0, keepdims=True)
@@ -471,7 +489,7 @@
     def _():
         padded = rows.shape[1]
         spread_table(z_block, z_table)
-        turned = jnp.dot(rows[...].reshape(groups * padded, BLOCK), z_table[...], **EXACT)
+        turned = product(rows[...].reshape(groups * padded, BLOCK), z_table[...])
         for part in range(BLOCK // NZ):
             along_z[part] = turned[:, part * LANES : (part + 1) * LANES]
         for plane in range(planes):
@@ -479,7 +497,7 @@
                 along_y[part * groups : (part + 1) * groups, plane * LANES : (plane + 1) * LANES] = along_z[
                     part, pl.ds(plane, groups, stride=padded), :
                 ]
-        waves = jnp.dot(y_table[...], along_y[...], **EXACT)
+        waves = product(y_table[...], along_y[...])
         peak = jnp.max(jnp.max(jnp.abs(waves), axis=1, keepdims=True), axis=0, keepdims=True)
         lift = power_over(peak)
         for part in range(chunks.shape[3] // LANES):
@@ -490,13 +508,13 @@
             for quarter in range(planes // 4):
                 start = member * planes + quarter * 4
                 for part in range(chunks.shape[3] // LANES):
-                    lanes = slice(part * LANES, (part + 1) * LANES)
-                    chunks[member, quarter, :, lanes] = sent[part, start : start + 4, :]
+                    tile = slice(part * LANES, (part + 1) * LANES)
+                    chunks[member, quarter, :, tile] = sent[part, start : start + 4, :]
 
 
 def finish(partial, below, above, occupations, z_table, y_table, members):
     planes, fields, cells = partial.shape
-    rim_spec = pl.BlockSpec((REACH, fields, CHUNK), lambda i: (0, 0, i))
+    rim_spec = pl.BlockSpec(memory_space=pltpu.VMEM)
     groups = cells // BLOCK
     padded = -(-planes // 8) * 8
     width = NY // members * LANES
@@ -504,19 +522,19 @@
     wave_shape = (members, planes // 4, 4, width)
     return pl.pallas_call(
         finish_kernel,
-        grid=(cells // CHUNK,),
+        grid=(cells // WIDE_CHUNK,),
         in_specs=[
             pl.BlockSpec(memory_space=pltpu.SMEM),
-            pl.BlockSpec((planes, fields, CHUNK), lambda i: (0, 0, i)),
+            pl.BlockSpec((planes, fields, WIDE_CHUNK), lambda i: (0, 0, i)),
             rim_spec,
             rim_spec,
             whole(z_table.shape),
             whole(y_table.shape),
         ],
-        out_specs=[pl.BlockSpec((2, planes, fields // 2, CHUNK), lambda i: (0, 0, 0, i)), whole(wave_shape)],
+        out_specs=[pl.BlockSpec((2, planes, fields // 2, WIDE_CHUNK), lambda i: (0, 0, 0, i)), pl.BlockSpec(memory_space=pltpu.VMEM)],
         out_shape=[
             jax.ShapeDtypeStruct((2, planes, fields // 2, cells), jnp.float32),
-            jax.ShapeDtypeStruct(wave_shape, jnp.float32),
+            pltpu.VMEM(wave_shape, jnp.float32),
         ],
         scratch_shapes=[
             pltpu.VMEM((BLOCK, BLOCK // NZ * LANES), jnp.float32),
@@ -544,8 +562,8 @@
         for band in range(1, members // blocks):
             total = total + unpacked(raw[band * length : (band + 1) * length, lanes])
         columns[:, lanes] = total
-    waves = jnp.dot(x_table[...], columns[...], **EXACT) * multiplier[...]
-    field = jnp.dot(back_table[...], waves, **EXACT)
+    waves = exact_product(x_table[...], columns[...]) * multiplier[...]
+    field = exact_product(back_table[...], waves)
     for index, values in enumerate((columns[...], field)):
         peak = jnp.max(jnp.max(jnp.abs(values), axis=1, keepdims=True), axis=0, keepdims=True)
         lift = power_over(peak)
@@ -563,7 +581,8 @@
     length = x_table.shape[0]
     return pl.pallas_call(
         column_kernel,
-        out_shape=jax.ShapeDtypeStruct((blocks, quarters, 4, 2 * width), jnp.float32),
+        out_shape=pltpu.VMEM((blocks, quarters, 4, 2 * width), jnp.float32),
+        out_specs=pl.BlockSpec(memory_space=pltpu.VMEM),
         scratch_shapes=[
             pltpu.VMEM((members * quarters * 4, width), jnp.float32),
             pltpu.VMEM((length, width), jnp.float32),
@@ -589,13 +608,13 @@
             for part in range(width // LANES):
                 block = raw[index * (width // LANES) + part, pl.ds(plane, members, stride=planes), :]
                 along_y[part * members : (part + 1) * members, plane * LANES : (plane + 1) * LANES] = unpacked(block)
-        waves = jnp.dot(y_back[...], along_y[...], **EXACT)
+        waves = product(y_back[...], along_y[...])
         for plane in range(planes):
             for part in range(BLOCK // NZ):
                 along_z[plane * groups : (plane + 1) * groups, part * LANES : (part + 1) * LANES] = waves[
                     part * groups : (part + 1) * groups, plane * LANES : (plane + 1) * LANES
                 ]
-        cells = lax.dot_general(along_z[...], z_table[...], (((1,), (1,)), ((), ())), **EXACT)
+        cells = product(along_z[...], z_table[...], 1)
         for tile in range(BLOCK // LANES):
             result[tile] = cells[:, tile * LANES : (tile + 1) * LANES]
         for group in range(groups):
@@ -672,15 +691,19 @@
     return return_waves(exchange(spread), jnp.asarray(y_table.T), jnp.asarray(z_table), cells)
 
 
+def in_place(x):
+    return pltpu.with_memory_space_constraint(x, pltpu.VMEM)
+
+
 def per_device_blocks(orbitals, potential, occupations):
     moved = orbitals.transpose(0, 2, 1, 3)
     table = plane_table()
     lower, upper = rim_copies(moved)
-    below = from_behind(upper, "space", 1)
-    above = from_behind(lower, "space", -1)
+    below = in_place(from_behind(upper, "space", 1))
+    above = in_place(from_behind(lower, "space", -1))
     partial, to_lower, to_upper = first_partial(moved, potential, table)
-    terms_below = from_behind(to_upper, "space", 1)
-    terms_above = from_behind(to_lower, "space", -1)
+    terms_below = in_place(from_behind(to_upper, "space", 1))
+    terms_above = in_place(from_behind(to_lower, "space", -1))
     partial = second_partial(partial, below, above, moved, potential, table)
     members = lax.axis_size("band") * lax.axis_size("space")
     tables = wave_tables(members, orbitals.shape[2] * lax.axis_size("space"))
@@ -694,7 +717,7 @@
 def per_device(orbitals, potential, occupations):
     _, count, planes, cells = orbitals.shape
     columns = NY % (lax.axis_size("space") * lax.axis_size("band"))
-    if planes < 2 * REACH or planes % 4 or count != 4 or cells % CHUNK or PERIOD % NZ or MARGIN != REACH * NZ or columns:
+    if planes < 2 * REACH or planes % 4 or count != 4 or cells % CHUNK or cells % WIDE_CHUNK or PERIOD % NZ or MARGIN != REACH * NZ or columns:
         return per_device_general(orbitals, potential, occupations)
     return per_device_blocks(orbitals, potential, occupations)
 

time: 96.8 us -> 88.1 us (0.910)
  Pallas kernels: 37.8 us -> 33.2 us
  local copies, waits for them, and re-layouts: 3.03 us -> 0.42 us
  other arithmetic: 5.84 us -> 4.4 us
    pallas_call x2, Pallas kernels: 11.6 us -> 8.64 us  [the longest x1 6.36 us: finish(): pl.pallas_call(finish_kernel, grid=(cells // WIDE_CHUNK,), in_specs=[pl.B...]
    unnamed x12 -> x6, local copies, waits for them, and re-layouts: 2.63 us -> 0.02 us
    pallas_call x1, Pallas kernels: 5.55 us -> 4.36 us  [return_waves(): pl.pallas_call(return_kernel, out_shape=[plane_shape, plane_shape], scrat...]
    convert_element_type x1, other arithmetic: 1.88 us -> 0.82 us  [density_and_field(): chunks.astype(jnp.float16)]
  transfers between devices with their start and end apart: 5 -> 5, of which waited for: 1 -> 1; matrix products, arithmetic and copies ran while one was open for 1% -> 2% of each run, Pallas kernels for 19% -> 20%
where the time goes in v2:
time: 88.1 us; the launch traced here: 87.6 us
  Pallas kernels  33.2 us (38%)
  starting transfers between devices  19.5 us (22%)
  blocking collectives  18.9 us (21%)
  waiting for transfers between devices  10.4 us (12%)
  other arithmetic  4.4 us (5%)
    all_to_all x1, blocking collectives, density_and_field(): lax.all_to_all(chunks.astype(jnp.float16), ('band', 'space'), split_axis=...  18.9 us
    all_to_all x1, waiting for transfers between devices, density_and_field(): lax.all_to_all(chunks.astype(jnp.float16), ('band', 'space'), split_axis=...  10.4 us
    ppermute x4, starting transfers between devices, from_behind(): return lax.ppermute(x, axis, pairs)  10.1 us
    pallas_call x1, Pallas kernels, second_partial(): pl.pallas_call(second_kernel, grid=(chunks + 1,), in_specs=[pl.BlockSpec(...  9.57 us
    all_to_all x1, starting transfers between devices, density_and_field(): lax.all_to_all(chunks.astype(jnp.float16), ('band', 'space'), split_axis=...  9.37 us
    pallas_call x1, Pallas kernels, first_partial(): pl.pallas_call(first_kernel, grid=(chunks,), in_specs=[pl.BlockSpec((2, p...  8.03 us
    pallas_call x1, Pallas kernels, finish(): pl.pallas_call(finish_kernel, grid=(cells // WIDE_CHUNK,), in_specs=[pl.B...  6.36 us
    pallas_call x1, Pallas kernels, return_waves(): pl.pallas_call(return_kernel, out_shape=[plane_shape, plane_shape], scrat...  4.36 us
  transfers between devices with their start and end apart: 5, of which 1 were waited for; matrix products, arithmetic and copies ran while one was open for 2% of the time, Pallas kernels for 20%

profile of v2, /device:TPU:0, one launch (start us, length us, event | category | flops | bytes accessed | tf_op | source)
XLA Modules:
  0.0 87.6 jit_solution(14789782717687452085)
XLA Ops:
  0.6 2.7 %rim_copies.1 = (bf16[4,8,9216]{2,1,0:T(8,128)(2,1)}, bf16[4,8,9216]{2,1,0:T(8,128)(2,1)}) custom-call(f32[2,12,4,9216]{3,2,1,0:T(4,128)} %bitcast.12), custom_call_target="tpu_custom_call" | custom-call | tf_op jit(solution)/shard_map/rim_copies/pallas_call | solution.py:211
  3.3 2.4 %collective-permute-start = (bf16[4,8,9216]{2,1,0:T(8,128)(2,1)}, bf16[4,8,9216]{2,1,0:T(8,128)(2,1)S(1)}, u32[]{:S(2)}, u32[]{:S(2)}) collective-permute-start(bf16[4,8,9216]{2,1,0:T(8,128)(2,1)} %get-tuple-element.13), channel_id=1, source_target_pairs={{0,1},{1,2},{2,3},{3,4},{4,5},{5,6},{6,7},{8,9},{9,10},{10,11},{11... | collective-permute-start | bytes 1769480 | tf_op jit(solution)/shard_map/ppermute | solution.py:25
  5.7 0.0 copy-start
  5.7 0.0 copy-start.1
  5.8 1.3 %collective-permute-start.1 = (bf16[4,8,9216]{2,1,0:T(8,128)(2,1)}, bf16[4,8,9216]{2,1,0:T(8,128)(2,1)S(1)}, u32[]{:S(2)}, u32[]{:S(2)}) collective-permute-start(bf16[4,8,9216]{2,1,0:T(8,128)(2,1)} %get-tuple-element.14), channel_id=1, source_target_pairs={{1,0},{2,1},{3,2},{4,3},{5,4},{6,5},{7,6},{9,8},{10,9},{11,10},{12... | collective-permute-start | bytes 1769480 | tf_op jit(solution)/shard_map/ppermute | solution.py:25
  7.1 8.0 %first_partial.1 = (f32[12,8,9216]{2,1,0:T(8,128)}, bf16[4,8,9216]{2,1,0:T(8,128)(2,1)S(1)}, bf16[4,8,9216]{2,1,0:T(8,128)(2,1)S(1)}) custom-call(f32[2,12,4,9216]{3,2,1,0:T(4,128)} %bitcast.13, f32[2,12,4,9216]{3,2,1,0:T(4,128)} %bitcast.14, f32[2,12,4,9216]{3,2,1,0:T(4,128)} %bitcast.15, f32[12,9216]{1,0:T(8,128)} %potential.3, ...), custom_call_target="tpu_custom_call" | custom-call | flops 100000000 | bytes 10000000 | tf_op jit(solution)/shard_map/first_partial/pallas_call | solution.py:285
  15.1 5.1 %collective-permute-start.2 = (bf16[4,8,9216]{2,1,0:T(8,128)(2,1)S(1)}, bf16[4,8,9216]{2,1,0:T(8,128)(2,1)S(1)}, u32[]{:S(2)}, u32[]{:S(2)}) collective-permute-start(bf16[4,8,9216]{2,1,0:T(8,128)(2,1)S(1)} %get-tuple-element.15), channel_id=1, source_target_pairs={{0,1},{1,2},{2,3},{3,4},{4,5},{5,6},{6,7},{8,9},{9,10},{10,11},{11... | collective-permute-start | bytes 1769480 | tf_op jit(solution)/shard_map/ppermute | solution.py:25
  20.2 1.3 %collective-permute-start.3 = (bf16[4,8,9216]{2,1,0:T(8,128)(2,1)S(1)}, bf16[4,8,9216]{2,1,0:T(8,128)(2,1)S(1)}, u32[]{:S(2)}, u32[]{:S(2)}) collective-permute-start(bf16[4,8,9216]{2,1,0:T(8,128)(2,1)S(1)} %get-tuple-element.16), channel_id=1, source_target_pairs={{1,0},{2,1},{3,2},{4,3},{5,4},{6,5},{7,6},{9,8},{10,9},{11,10},{12... | collective-permute-start | bytes 1769480 | tf_op jit(solution)/shard_map/ppermute | solution.py:25
  21.5 0.0 copy-done
  21.5 0.1 dynamic_slice.3
  21.6 0.6 iota_compare_fusion
  22.2 0.0 copy-done.1
  22.2 0.0 collective-permute-done.below
  22.2 0.0 collective-permute-done.1.above
  22.2 9.6 %second_partial.1.partial = f32[12,8,9216]{2,1,0:T(8,128)} custom-call(f32[12,8,9216]{2,1,0:T(8,128)} %get-tuple-element.12.partial, bf16[4,8,9216]{2,1,0:T(8,128)(2,1)S(1)} %collective-permute-done.below, bf16[4,8,9216]{2,1,0:T(8,128)(2,1)S(1)} %collective-permute-done.1.above, f32[2,12,4,9216]{3,2,1,0:T(4,128)} %bitcast.16, f32[12,9216]{1,0:T(8,128)} %potential.3, ...), custom_call_target="tpu_custom_call" | custom-call | flops 100000000 | bytes 10000000 | tf_op jit(solution)/shard_map/second_partial/pallas_call | solution.py:391
  31.8 0.0 copy-start.2
  31.8 0.0 collective-permute-done.2.below
  31.8 0.0 collective-permute-done.3.above
  31.8 6.4 %finish.1 = (f32[2,12,4,9216]{3,2,1,0:T(4,128)}, f32[32,3,4,384]{3,2,1,0:T(4,128)S(1)}) custom-call(f32[4]{0:T(128)} %shares.1, f32[12,8,9216]{2,1,0:T(8,128)} %second_partial.1.partial, bf16[4,8,9216]{2,1,0:T(8,128)(2,1)S(1)} %collective-permute-done.2.below, bf16[4,8,9216]{2,1,0:T(8,128)(2,1)S(1)} %collective-permute-done.3.above, ...), custom_call_target="tpu_custom_call" | custom-call | tf_op jit(solution)/shard_map/finish/pallas_call | solution.py:523
  38.2 0.8 convert_element_type.12
  39.0 9.4 %all-to-all-start = ((f16[32,3,4,384]{3,2,1,0:T(4,128)(2,1)}), f16[32,3,4,384]{3,2,1,0:T(4,128)(2,1)S(1)}, u32[]{:S(2)}, u32[]{:S(2)}) async-start(f16[32,3,4,384]{3,2,1,0:T(4,128)(2,1)} %convert_element_type.12), calls=%async_computation | async-start | bytes 589824 | tf_op jit(solution)/shard_map/all_to_all | solution.py:675
  48.3 0.0 copy-done.2
  48.4 0.1 broadcast_add_fusion
  48.4 0.2 add.49
  48.6 0.7 fusion.1.multiplier
  49.3 10.4 %all-to-all-done = f16[32,3,4,384]{3,2,1,0:T(4,128)(2,1)S(1)} async-done(((f16[32,3,4,384]{3,2,1,0:T(4,128)(2,1)}), f16[32,3,4,384]{3,2,1,0:T(4,128)(2,1)S(1)}, u32[]{:S(2)}, u32[]{:S(2)}) %all-to-all-start) | async-done | bytes 294944 | tf_op jit(solution)/shard_map/all_to_all | solution.py:675
  59.7 0.9 %convert_element_type.13.arrived = f32[32,3,4,384]{3,2,1,0:T(4,128)} convert(f16[32,3,4,384]{3,2,1,0:T(4,128)(2,1)S(1)} %all-to-all-done) | non-fusion elementwise | flops 147456 | bytes 884736 | tf_op jit(solution)/shard_map/convert_element_type | solution.py:677
  60.7 2.3 %column_waves.1 = f32[8,3,4,768]{3,2,1,0:T(4,128)S(1)} custom-call(f32[32,3,4,384]{3,2,1,0:T(4,128)} %convert_element_type.13.arrived, f32[96,384]{1,0:T(8,128)} %fusion.1.multiplier, f32[96,96]{1,0:T(8,128)} %constant.45.clone.x_table, f32[96,96]{1,0:T(8,128)} %constant.46.clone.back_table), custom_call_target="tpu_custom_call" | custom-call | tf_op jit(solution)/shard_map/column_waves/pallas_call | solution.py:582
  62.9 0.1 convert_element_type.14
  63.0 0.2 broadcast_in_dim.8
  63.2 18.9 %all_to_all.10 = f16[32,3,4,768]{3,2,1,0:T(4,128)(2,1)S(1)} all-to-all(f16[32,3,4,768]{3,2,1,0:T(4,128)(2,1)S(1)} %bitcast.17), channel_id=1, replica_groups=mesh['band'=4,'space'=8] {'band','space'}, dimensions={0} | all-to-all | bytes 1179648 | tf_op jit(solution)/shard_map/all_to_all | solution.py:675
  82.1 1.2 %convert_element_type.15.arrived = f32[32,3,4,768]{3,2,1,0:T(4,128)} convert(f16[32,3,4,768]{3,2,1,0:T(4,128)(2,1)S(1)} %all_to_all.10) | non-fusion elementwise | flops 294912 | bytes 1769472 | tf_op jit(solution)/shard_map/convert_element_type | solution.py:677
  83.3 4.4 %return_waves.1 = (f32[12,9216]{1,0:T(8,128)}, f32[12,9216]{1,0:T(8,128)}) custom-call(f32[32,3,4,768]{3,2,1,0:T(4,128)} %convert_element_type.15.arrived, f32[96,96]{1,0:T(8,128)} %constant.47.clone.y_back, f32[96,128]{1,0:T(8,128)} %constant.41.clone.z_block), custom_call_target="tpu_custom_call" | custom-call | tf_op jit(solution)/shard_map/return_waves/pallas_call | solution.py:631
  (2 shorter events, 0.0 us)
Async XLA Ops:
  3.3 18.9 %collective-permute-start = (bf16[4,8,9216]{2,1,0:T(8,128)(2,1)}, bf16[4,8,9216]{2,1,0:T(8,128)(2,1)S(1)}, u32[]{:S(2)}, u32[]{:S(2)}) collective-permute-start(bf16[4,8,9216]{2,1,0:T(8,128)(2,1)} %get-tuple-element.13), channel_id=1, source_target_pairs={{0,1},{1,2},{2,3},{3,4},{4,5},{5,6},{6,7},{8,9},{9,10},{10,11},{11... | collective-permute-start | bytes 1769480 | tf_op jit(solution)/shard_map/ppermute | solution.py:25
  5.7 15.8 %copy-start = (f32[96]{0:T(128)S(1)}, f32[96]{0:T(128)}, u32[]{:S(2)}) copy-start(f32[96]{0:T(128)} %constant.43.clone) | copy-start | bytes 1156
  5.7 16.5 %copy-start.1 = (f32[128]{0:T(128)S(1)}, f32[128]{0:T(128)}, u32[]{:S(2)}) copy-start(f32[128]{0:T(128)} %constant.44.clone) | copy-start | bytes 1540
  5.8 16.4 %collective-permute-start.1 = (bf16[4,8,9216]{2,1,0:T(8,128)(2,1)}, bf16[4,8,9216]{2,1,0:T(8,128)(2,1)S(1)}, u32[]{:S(2)}, u32[]{:S(2)}) collective-permute-start(bf16[4,8,9216]{2,1,0:T(8,128)(2,1)} %get-tuple-element.14), channel_id=1, source_target_pairs={{1,0},{2,1},{3,2},{4,3},{5,4},{6,5},{7,6},{9,8},{10,9},{11,10},{12... | collective-permute-start | bytes 1769480 | tf_op jit(solution)/shard_map/ppermute | solution.py:25
  15.1 16.7 %collective-permute-start.2 = (bf16[4,8,9216]{2,1,0:T(8,128)(2,1)S(1)}, bf16[4,8,9216]{2,1,0:T(8,128)(2,1)S(1)}, u32[]{:S(2)}, u32[]{:S(2)}) collective-permute-start(bf16[4,8,9216]{2,1,0:T(8,128)(2,1)S(1)} %get-tuple-element.15), channel_id=1, source_target_pairs={{0,1},{1,2},{2,3},{3,4},{4,5},{5,6},{6,7},{8,9},{9,10},{10,11},{11... | collective-permute-start | bytes 1769480 | tf_op jit(solution)/shard_map/ppermute | solution.py:25
  20.2 11.6 %collective-permute-start.3 = (bf16[4,8,9216]{2,1,0:T(8,128)(2,1)S(1)}, bf16[4,8,9216]{2,1,0:T(8,128)(2,1)S(1)}, u32[]{:S(2)}, u32[]{:S(2)}) collective-permute-start(bf16[4,8,9216]{2,1,0:T(8,128)(2,1)S(1)} %get-tuple-element.16), channel_id=1, source_target_pairs={{1,0},{2,1},{3,2},{4,3},{5,4},{6,5},{7,6},{9,8},{10,9},{11,10},{12... | collective-permute-start | bytes 1769480 | tf_op jit(solution)/shard_map/ppermute | solution.py:25
  31.8 16.6 %copy-start.2 = (pred[128]{0:T(512)(128)(4,1)S(1)}, pred[128]{0:T(512)(128)(4,1)}, u32[]{:S(2)}) copy-start(pred[128]{0:T(512)(128)(4,1)} %iota_compare_fusion) | copy-start | bytes 388
  39.0 20.8 %all-to-all-start = ((f16[32,3,4,384]{3,2,1,0:T(4,128)(2,1)}), f16[32,3,4,384]{3,2,1,0:T(4,128)(2,1)S(1)}, u32[]{:S(2)}, u32[]{:S(2)}) async-start(f16[32,3,4,384]{3,2,1,0:T(4,128)(2,1)} %convert_element_type.12), calls=%async_computation | async-start | bytes 589824 | tf_op jit(solution)/shard_map/all_to_all | solution.py:675

commit v3 on v2

--- a/solution.py
+++ b/solution.py
@@ -165,6 +165,7 @@
 PERIOD = 768
 CHUNK = 2304
 WIDE_CHUNK = 4608
+KERNEL_MEMORY = 36 * 2**20
 WINDOW = 1024
 TILE = 256
 MARGIN = 384
@@ -217,6 +218,7 @@
             pltpu.VMEM((2, 2, REACH, count, cells), jnp.float32),
             pltpu.SemaphoreType.DMA((2,)),
         ],
+        compiler_params=pltpu.CompilerParams(vmem_limit_bytes=KERNEL_MEMORY),
         name="rim_copies",
     )(moved)
 
@@ -264,7 +266,7 @@
                 - (0.5 / energy_scale / TABLE_SCALE) * in_plane[rows]
                 - across(lambda at: values[fields * at : fields * (at + 1), lanes], plane, planes)
             )
-            partial[plane, :, lanes] = result
+            partial[plane, :, pl.ds(pl.multiple_of(step * CHUNK + phase * TILE, TILE), TILE)] = result
             results.append(result)
         for rim, into, order in ((to_upper, "up", results[::-1]), (to_lower, "down", results)):
             for plane in range(REACH):
@@ -295,13 +297,14 @@
             pl.BlockSpec((planes, CHUNK), lambda i: (0, i)),
             pl.BlockSpec(table.shape, lambda i: (0, 0, 0)),
         ],
-        out_specs=[pl.BlockSpec((planes, fields, CHUNK), lambda i: (0, 0, i)), rim_spec, rim_spec],
-        out_shape=[jax.ShapeDtypeStruct((planes, fields, cells), jnp.float32), rim, rim],
+        out_specs=[rim_spec, rim_spec, rim_spec],
+        out_shape=[pltpu.VMEM((planes, fields, cells), jnp.float32), rim, rim],
         scratch_shapes=[
             pltpu.VMEM((planes * fields, CHUNK + 2 * MARGIN), jnp.bfloat16),
             pltpu.VMEM((planes * fields, CHUNK), jnp.float32),
         ],
         cost_estimate=pl.CostEstimate(flops=10**8, transcendentals=0, bytes_accessed=10**7),
+        compiler_params=pltpu.CompilerParams(vmem_limit_bytes=KERNEL_MEMORY),
         name="first_partial",
     )(moved, moved, moved, potential, table)
 
@@ -337,7 +340,7 @@
         base = pl.multiple_of(step * CHUNK, TILE)
         for plane in range(planes):
             rows = slice(fields * plane, fields * (plane + 1))
-            first = partial[plane]
+            first = partial[plane, :, pl.ds(base, CHUNK)]
             for offset in range(1, REACH + 1):
                 if plane - offset < 0:
                     first = first - half_scale * stencil_coeffs[offset] * below[REACH + plane - offset, :, pl.ds(base, CHUNK)].astype(jnp.float32)
@@ -378,7 +381,7 @@
                 if mirrored < REACH:
                     total = sum(float(gain * rim[mirrored, at]) * origin[planes - 1 - at] for at in range(REACH))
                     result = result + flags[1] * total
-                out[plane, :, lanes] = result
+                out[plane, :, pl.ds(start, TILE)] = result
 
 
 def second_partial(partial, below, above, moved, potential, table):
@@ -392,20 +395,21 @@
         second_kernel,
         grid=(chunks + 1,),
         in_specs=[
-            pl.BlockSpec((planes, fields, CHUNK), lambda i: (0, 0, ahead(i))),
+            rim_spec,
             rim_spec,
             rim_spec,
             pl.BlockSpec((2, planes, count, CHUNK), lambda i: (0, 0, 0, behind(i))),
             pl.BlockSpec((planes, CHUNK), lambda i: (0, behind(i))),
             pl.BlockSpec(table.shape, lambda i: (0, 0, 0)),
         ],
-        out_specs=pl.BlockSpec((planes, fields, CHUNK), lambda i: (0, 0, behind(i))),
-        out_shape=jax.ShapeDtypeStruct((planes, fields, cells), jnp.float32),
+        out_specs=rim_spec,
+        out_shape=pltpu.VMEM((planes, fields, cells), jnp.float32),
         scratch_shapes=[
             pltpu.VMEM((planes * fields, cells + 2 * MARGIN), jnp.bfloat16),
             pltpu.VMEM((planes * fields, cells), jnp.float32),
         ],
         cost_estimate=pl.CostEstimate(flops=10**8, transcendentals=0, bytes_accessed=10**7),
+        compiler_params=pltpu.CompilerParams(vmem_limit_bytes=KERNEL_MEMORY),
         name="second_partial",
     )(partial, below, above, moved, potential, table)
 
@@ -474,7 +478,7 @@
         weight = jnp.where(field == at, shares[at], weight)
     weight = weight * (1.0 / (count * lax.axis_size("band")))
     for plane in range(planes):
-        value = partial[plane]
+        value = partial[plane, :, lanes]
         if plane < REACH:
             value = value + gain * below[plane, :, lanes].astype(jnp.float32)
         if planes - 1 - plane < REACH:
@@ -525,7 +529,7 @@
         grid=(cells // WIDE_CHUNK,),
         in_specs=[
             pl.BlockSpec(memory_space=pltpu.SMEM),
-            pl.BlockSpec((planes, fields, WIDE_CHUNK), lambda i: (0, 0, i)),
+            rim_spec,
             rim_spec,
             rim_spec,
             whole(z_table.shape),
@@ -543,6 +547,7 @@
             pltpu.VMEM((NY, planes * LANES), jnp.float32),
             pltpu.VMEM((width // LANES, members * planes, LANES), jnp.float32),
         ],
+        compiler_params=pltpu.CompilerParams(vmem_limit_bytes=KERNEL_MEMORY),
         name="finish",
     )(occupations, partial, below, above, z_table, y_table)
 
@@ -588,6 +593,7 @@
             pltpu.VMEM((length, width), jnp.float32),
             pltpu.VMEM((length, 2 * width), jnp.float32),
         ],
+        compiler_params=pltpu.CompilerParams(vmem_limit_bytes=KERNEL_MEMORY),
         name="column_waves",
     )(arrived, multiplier, jnp.asarray(x_table), jnp.asarray(x_table.T))
 
@@ -638,6 +644,7 @@
             pltpu.VMEM((planes * groups, BLOCK // NZ * LANES), jnp.float32),
             pltpu.VMEM((BLOCK // LANES, planes * groups, LANES), jnp.float32),
         ],
+        compiler_params=pltpu.CompilerParams(vmem_limit_bytes=KERNEL_MEMORY),
         name="return_waves",
     )(arrived, y_table, z_table)
 
@@ -680,11 +687,10 @@
     squares = (
         jnp.asarray(x_squares, jnp.float32)[:, None, None]
         + lax.dynamic_slice_in_dim(jnp.asarray(y_squares, jnp.float32), place, rows)[None, :, None]
-        + jnp.asarray(np.pad(z_squares, (0, LANES - NZ)), jnp.float32)[None, None, :]
-    )
-    used = lax.broadcasted_iota(jnp.int32, squares.shape, 2) < NZ
+        + jnp.asarray(np.pad(z_squares, (0, LANES - NZ), constant_values=-1e9), jnp.float32)[None, None, :]
+    )
     multiplier = jnp.where(
-        (squares > 0) & used, 4.0 * math.pi / jnp.where(squares > 0, squares, 1.0), 0.0
+        squares > 0, 4.0 * math.pi / jnp.where(squares > 0, squares, 1.0), 0.0
     ).reshape(-1, width)
     both = column_waves(exchange(waves), multiplier, x_table, blocks)
     spread = jnp.broadcast_to(both.astype(jnp.float16)[None], (bands, *both.shape)).reshape(members, *both.shape[1:])
@@ -696,8 +702,10 @@
 
 
 def per_device_blocks(orbitals, potential, occupations):
-    moved = orbitals.transpose(0, 2, 1, 3)
-    table = plane_table()
+    moved, potential, table = (
+        pltpu.with_memory_space_constraint(x, pltpu.HBM)
+        for x in (orbitals.transpose(0, 2, 1, 3), potential, plane_table())
+    )
     lower, upper = rim_copies(moved)
     below = in_place(from_behind(upper, "space", 1))
     above = in_place(from_behind(lower, "space", -1))

time: 88.1 us -> 83.7 us (0.950)
  Pallas kernels: 33.2 us -> 29.3 us
  other arithmetic: 4.4 us -> 1.29 us
  starting transfers between devices: 19.5 us -> 21.4 us
    convert_element_type x2, other arithmetic: 2.15 us -> 0.31 us  [density_and_field(): exchange = lambda chunks: lax.all_to_all(chunks.astype(jnp.float16), ('ba...]
    pallas_call x1, Pallas kernels: 4.36 us -> 3.07 us  [return_waves(): pl.pallas_call(return_kernel, out_shape=[plane_shape, plane_shape], scrat...]
    pallas_call x1, Pallas kernels: 2.28 us -> 1.14 us  [column_waves(): pl.pallas_call(column_kernel, out_shape=pltpu.VMEM((blocks, quarters, 4,...]
    all_to_all x1, starting transfers between devices: 9.37 us -> 10.5 us  [density_and_field(): lax.all_to_all(chunks.astype(jnp.float16), ('band', 'space'), split_axis=...]
    pallas_call x1, Pallas kernels: 9.57 us -> 8.54 us  [second_partial(): pl.pallas_call(second_kernel, grid=(chunks + 1,), in_specs=[rim_spec, rim...]
  transfers between devices with their start and end apart: 5 -> 5, of which waited for: 1 -> 1; matrix products, arithmetic and copies ran while one was open for 2% -> 0% of each run, Pallas kernels for 20% -> 20%
where the time goes in v3:
time: 83.7 us; the launch traced here: 83.3 us
  Pallas kernels  29.3 us (35%)
  starting transfers between devices  21.4 us (26%)
  blocking collectives  18.9 us (23%)
  waiting for transfers between devices  11.1 us (13%)
  other arithmetic  1.29 us (2%)
  between operations  0.88 us (1%)
    all_to_all x1, blocking collectives, density_and_field(): lax.all_to_all(chunks.astype(jnp.float16), ('band', 'space'), split_axis=...  18.9 us
    all_to_all x1, waiting for transfers between devices, density_and_field(): lax.all_to_all(chunks.astype(jnp.float16), ('band', 'space'), split_axis=...  11.1 us
    ppermute x4, starting transfers between devices, from_behind(): return lax.ppermute(x, axis, pairs)  10.9 us
    all_to_all x1, starting transfers between devices, density_and_field(): lax.all_to_all(chunks.astype(jnp.float16), ('band', 'space'), split_axis=...  10.5 us
    pallas_call x1, Pallas kernels, second_partial(): pl.pallas_call(second_kernel, grid=(chunks + 1,), in_specs=[rim_spec, rim...  8.54 us
    pallas_call x1, Pallas kernels, first_partial(): pl.pallas_call(first_kernel, grid=(chunks,), in_specs=[pl.BlockSpec((2, p...  7.78 us
    pallas_call x1, Pallas kernels, finish(): pl.pallas_call(finish_kernel, grid=(cells // WIDE_CHUNK,), in_specs=[pl.B...  6.11 us
    pallas_call x1, Pallas kernels, return_waves(): pl.pallas_call(return_kernel, out_shape=[plane_shape, plane_shape], scrat...  3.07 us
  transfers between devices with their start and end apart: 5, of which 1 were waited for; matrix products, arithmetic and copies ran while one was open for 0% of the time, Pallas kernels for 20%

profile of v3, /device:TPU:0, one launch (start us, length us, event | category | flops | bytes accessed | tf_op | source)
XLA Modules:
  0.0 83.3 jit_solution(1138930183443935212)
XLA Ops:
  0.6 2.7 %rim_copies.1 = (bf16[4,8,9216]{2,1,0:T(8,128)(2,1)}, bf16[4,8,9216]{2,1,0:T(8,128)(2,1)}) custom-call(f32[2,12,4,9216]{3,2,1,0:T(4,128)} %bitcast.10), custom_call_target="tpu_custom_call" | custom-call | tf_op jit(solution)/shard_map/rim_copies/pallas_call | solution.py:212
  3.3 3.2 %collective-permute-start = (bf16[4,8,9216]{2,1,0:T(8,128)(2,1)}, bf16[4,8,9216]{2,1,0:T(8,128)(2,1)}, u32[]{:S(2)}, u32[]{:S(2)}) collective-permute-start(bf16[4,8,9216]{2,1,0:T(8,128)(2,1)} %get-tuple-element.13), channel_id=1, source_target_pairs={{0,1},{1,2},{2,3},{3,4},{4,5},{5,6},{6,7},{8,9},{9,10},{10,11},{11... | collective-permute-start | bytes 1769480 | tf_op jit(solution)/shard_map/ppermute | solution.py:25
  6.5 0.0 copy-start.7
  6.5 1.4 %collective-permute-start.1 = (bf16[4,8,9216]{2,1,0:T(8,128)(2,1)}, bf16[4,8,9216]{2,1,0:T(8,128)(2,1)}, u32[]{:S(2)}, u32[]{:S(2)}) collective-permute-start(bf16[4,8,9216]{2,1,0:T(8,128)(2,1)} %get-tuple-element.14), channel_id=1, source_target_pairs={{1,0},{2,1},{3,2},{4,3},{5,4},{6,5},{7,6},{9,8},{10,9},{11,10},{12... | collective-permute-start | bytes 1769480 | tf_op jit(solution)/shard_map/ppermute | solution.py:25
  8.0 7.8 %first_partial.1 = (f32[12,8,9216]{2,1,0:T(8,128)S(1)}, bf16[4,8,9216]{2,1,0:T(8,128)(2,1)}, bf16[4,8,9216]{2,1,0:T(8,128)(2,1)}) custom-call(f32[2,12,4,9216]{3,2,1,0:T(4,128)} %bitcast.11, f32[2,12,4,9216]{3,2,1,0:T(4,128)} %bitcast.12, f32[2,12,4,9216]{3,2,1,0:T(4,128)} %bitcast.13, f32[12,9216]{1,0:T(8,128)} %potential.3, ...), custom_call_target="tpu_custom_call" | custom-call | flops 100000000 | bytes 10000000 | tf_op jit(solution)/shard_map/first_partial/pallas_call | solution.py:287
  15.7 5.0 %collective-permute-start.2 = (bf16[4,8,9216]{2,1,0:T(8,128)(2,1)}, bf16[4,8,9216]{2,1,0:T(8,128)(2,1)}, u32[]{:S(2)}, u32[]{:S(2)}) collective-permute-start(bf16[4,8,9216]{2,1,0:T(8,128)(2,1)} %get-tuple-element.15), channel_id=1, source_target_pairs={{0,1},{1,2},{2,3},{3,4},{4,5},{5,6},{6,7},{8,9},{9,10},{10,11},{11... | collective-permute-start | bytes 1769480 | tf_op jit(solution)/shard_map/ppermute | solution.py:25
  20.7 1.3 %collective-permute-start.3 = (bf16[4,8,9216]{2,1,0:T(8,128)(2,1)}, bf16[4,8,9216]{2,1,0:T(8,128)(2,1)}, u32[]{:S(2)}, u32[]{:S(2)}) collective-permute-start(bf16[4,8,9216]{2,1,0:T(8,128)(2,1)} %get-tuple-element.16), channel_id=1, source_target_pairs={{1,0},{2,1},{3,2},{4,3},{5,4},{6,5},{7,6},{9,8},{10,9},{11,10},{12... | collective-permute-start | bytes 1769480 | tf_op jit(solution)/shard_map/ppermute | solution.py:25
  22.0 0.0 copy-done.7
  22.0 0.1 dynamic_slice.3
  22.1 0.0 collective-permute-done.below
  22.1 0.0 collective-permute-done.1.above
  22.1 0.0 copy-start
  22.1 0.0 copy-start.2
  22.1 0.0 copy-start.6
  22.2 8.5 %second_partial.1.partial = f32[12,8,9216]{2,1,0:T(8,128)S(1)} custom-call(f32[12,8,9216]{2,1,0:T(8,128)S(1)} %get-tuple-element.12.partial, bf16[4,8,9216]{2,1,0:T(8,128)(2,1)} %collective-permute-done.below, bf16[4,8,9216]{2,1,0:T(8,128)(2,1)} %collective-permute-done.1.above, f32[2,12,4,9216]{3,2,1,0:T(4,128)} %bitcast.14, f32[12,9216]{1,0:T(8,128)} %potential.3, ...), custom_call_target="tpu_custom_call" | custom-call | flops 100000000 | bytes 10000000 | tf_op jit(solution)/shard_map/second_partial/pallas_call | solution.py:394
  30.7 0.0 copy-start.8
  30.7 0.0 copy-start.4
  30.7 0.0 copy-start.5
  30.7 0.0 collective-permute-done.2.below
  30.7 0.0 collective-permute-done.3.above
  30.8 0.0 copy-done
  30.8 0.0 copy-done.2
  30.8 0.0 copy-done.6
  30.8 6.1 %finish.1 = (f32[2,12,4,9216]{3,2,1,0:T(4,128)}, f32[32,3,4,384]{3,2,1,0:T(4,128)S(1)}) custom-call(f32[4]{0:T(128)S(1)} %copy-done.6, f32[12,8,9216]{2,1,0:T(8,128)S(1)} %second_partial.1.partial, bf16[4,8,9216]{2,1,0:T(8,128)(2,1)} %collective-permute-done.2.below, bf16[4,8,9216]{2,1,0:T(8,128)(2,1)} %collective-permute-done.3.above, ...), custom_call_target="tpu_custom_call" | custom-call | tf_op jit(solution)/shard_map/finish/pallas_call | solution.py:527
  36.9 0.8 convert_element_type.12
  37.7 10.5 %all-to-all-start = ((f16[32,3,4,384]{3,2,1,0:T(4,128)(2,1)}), f16[32,3,4,384]{3,2,1,0:T(4,128)(2,1)S(1)}, u32[]{:S(2)}, u32[]{:S(2)}) async-start(f16[32,3,4,384]{3,2,1,0:T(4,128)(2,1)} %convert_element_type.12), calls=%async_computation | async-start | bytes 589824 | tf_op jit(solution)/shard_map/all_to_all | solution.py:682
  48.2 0.0 copy-done.8
  48.2 0.0 copy-start.1
  48.2 0.0 copy-start.3
  48.2 0.1 broadcast_add_fusion
  48.3 0.2 add.49
  48.5 11.1 %all-to-all-done = f16[32,3,4,384]{3,2,1,0:T(4,128)(2,1)S(1)} async-done(((f16[32,3,4,384]{3,2,1,0:T(4,128)(2,1)}), f16[32,3,4,384]{3,2,1,0:T(4,128)(2,1)S(1)}, u32[]{:S(2)}, u32[]{:S(2)}) %all-to-all-start) | async-done | bytes 294944 | tf_op jit(solution)/shard_map/all_to_all | solution.py:682
  59.6 0.1 convert_element_type.13.arrived
  59.7 0.0 copy-done.4
  59.7 0.0 copy-done.5
  59.7 1.1 %column_waves.1 = f32[8,3,4,768]{3,2,1,0:T(4,128)S(1)} custom-call(f32[32,3,4,384]{3,2,1,0:T(4,128)S(1)} %convert_element_type.13.arrived, f32[96,384]{1,0:T(8,128)S(1)} %compare_select_fusion.multiplier, f32[96,96]{1,0:T(8,128)S(1)} %copy-done.4, f32[96,96]{1,0:T(8,128)S(1)} %copy-done.5), custom_call_target="tpu_custom_call" | custom-call | tf_op jit(solution)/shard_map/column_waves/pallas_call | solution.py:587
  60.9 0.1 convert_element_type.14
  60.9 0.2 broadcast_in_dim.8
  61.1 18.9 %all_to_all.10 = f16[32,3,4,768]{3,2,1,0:T(4,128)(2,1)S(1)} all-to-all(f16[32,3,4,768]{3,2,1,0:T(4,128)(2,1)S(1)} %bitcast.15), channel_id=1, replica_groups=mesh['band'=4,'space'=8] {'band','space'}, dimensions={0} | all-to-all | bytes 1179648 | tf_op jit(solution)/shard_map/all_to_all | solution.py:682
  80.0 0.2 convert_element_type.15.arrived
  80.2 0.0 copy-done.1
  80.2 0.0 copy-done.3
  80.2 3.1 %return_waves.1 = (f32[12,9216]{1,0:T(8,128)}, f32[12,9216]{1,0:T(8,128)}) custom-call(f32[32,3,4,768]{3,2,1,0:T(4,128)S(1)} %convert_element_type.15.arrived, f32[96,96]{1,0:T(8,128)S(1)} %copy-done.3, f32[96,128]{1,0:T(8,128)S(1)} %copy-done.1), custom_call_target="tpu_custom_call" | custom-call | tf_op jit(solution)/shard_map/return_waves/pallas_call | solution.py:637
  (2 shorter events, 0.0 us)
Async XLA Ops:
  3.3 18.8 %collective-permute-start = (bf16[4,8,9216]{2,1,0:T(8,128)(2,1)}, bf16[4,8,9216]{2,1,0:T(8,128)(2,1)}, u32[]{:S(2)}, u32[]{:S(2)}) collective-permute-start(bf16[4,8,9216]{2,1,0:T(8,128)(2,1)} %get-tuple-element.13), channel_id=1, source_target_pairs={{0,1},{1,2},{2,3},{3,4},{4,5},{5,6},{6,7},{8,9},{9,10},{10,11},{11... | collective-permute-start | bytes 1769480 | tf_op jit(solution)/shard_map/ppermute | solution.py:25
  6.5 15.5 %copy-start.7 = (f32[96]{0:T(128)S(1)}, f32[96]{0:T(128)}, u32[]{:S(2)}) copy-start(f32[96]{0:T(128)} %constant.42.clone) | copy-start | bytes 1156
  6.5 15.6 %collective-permute-start.1 = (bf16[4,8,9216]{2,1,0:T(8,128)(2,1)}, bf16[4,8,9216]{2,1,0:T(8,128)(2,1)}, u32[]{:S(2)}, u32[]{:S(2)}) collective-permute-start(bf16[4,8,9216]{2,1,0:T(8,128)(2,1)} %get-tuple-element.14), channel_id=1, source_target_pairs={{1,0},{2,1},{3,2},{4,3},{5,4},{6,5},{7,6},{9,8},{10,9},{11,10},{12... | collective-permute-start | bytes 1769480 | tf_op jit(solution)/shard_map/ppermute | solution.py:25
  15.7 15.0 %collective-permute-start.2 = (bf16[4,8,9216]{2,1,0:T(8,128)(2,1)}, bf16[4,8,9216]{2,1,0:T(8,128)(2,1)}, u32[]{:S(2)}, u32[]{:S(2)}) collective-permute-start(bf16[4,8,9216]{2,1,0:T(8,128)(2,1)} %get-tuple-element.15), channel_id=1, source_target_pairs={{0,1},{1,2},{2,3},{3,4},{4,5},{5,6},{6,7},{8,9},{9,10},{10,11},{11... | collective-permute-start | bytes 1769480 | tf_op jit(solution)/shard_map/ppermute | solution.py:25
  20.7 10.0 %collective-permute-start.3 = (bf16[4,8,9216]{2,1,0:T(8,128)(2,1)}, bf16[4,8,9216]{2,1,0:T(8,128)(2,1)}, u32[]{:S(2)}, u32[]{:S(2)}) collective-permute-start(bf16[4,8,9216]{2,1,0:T(8,128)(2,1)} %get-tuple-element.16), channel_id=1, source_target_pairs={{1,0},{2,1},{3,2},{4,3},{5,4},{6,5},{7,6},{9,8},{10,9},{11,10},{12... | collective-permute-start | bytes 1769480 | tf_op jit(solution)/shard_map/ppermute | solution.py:25
  22.1 8.6 %copy-start = (f32[96,128]{1,0:T(8,128)S(1)}, f32[96,128]{1,0:T(8,128)}, u32[]{:S(2)}) copy-start(f32[96,128]{1,0:T(8,128)} %constant.40.clone.z_block) | copy-start | bytes 147460
  22.1 8.6 %copy-start.2 = (f32[96,96]{1,0:T(8,128)S(1)}, f32[96,96]{1,0:T(8,128)}, u32[]{:S(2)}) copy-start(f32[96,96]{1,0:T(8,128)} %constant.41.clone.y_table) | copy-start | bytes 110596
  22.1 8.6 %copy-start.6 = (f32[4]{0:T(128)S(1)}, f32[4]{0:T(128)}, u32[]{:S(2)}) copy-start(f32[4]{0:T(128)} %shares.1) | copy-start | bytes 52
  30.7 17.5 %copy-start.8 = (f32[128]{0:T(128)S(1)}, f32[128]{0:T(128)}, u32[]{:S(2)}) copy-start(f32[128]{0:T(128)} %constant.43.clone) | copy-start | bytes 1540
  30.7 29.0 %copy-start.4 = (f32[96,96]{1,0:T(8,128)S(1)}, f32[96,96]{1,0:T(8,128)}, u32[]{:S(2)}) copy-start(f32[96,96]{1,0:T(8,128)} %constant.44.clone.x_table) | copy-start | bytes 110596
  30.7 29.0 %copy-start.5 = (f32[96,96]{1,0:T(8,128)S(1)}, f32[96,96]{1,0:T(8,128)}, u32[]{:S(2)}) copy-start(f32[96,96]{1,0:T(8,128)} %constant.45.clone.back_table) | copy-start | bytes 110596
  37.7 21.9 %all-to-all-start = ((f16[32,3,4,384]{3,2,1,0:T(4,128)(2,1)}), f16[32,3,4,384]{3,2,1,0:T(4,128)(2,1)S(1)}, u32[]{:S(2)}, u32[]{:S(2)}) async-start(f16[32,3,4,384]{3,2,1,0:T(4,128)(2,1)} %convert_element_type.12), calls=%async_computation | async-start | bytes 589824 | tf_op jit(solution)/shard_map/all_to_all | solution.py:682
  48.2 32.0 %copy-start.1 = (f32[96,128]{1,0:T(8,128)S(1)}, f32[96,128]{1,0:T(8,128)}, u32[]{:S(2)}) copy-start(f32[96,128]{1,0:T(8,128)} %constant.40.clone.z_block) | copy-start | bytes 147460
  48.2 32.0 %copy-start.3 = (f32[96,96]{1,0:T(8,128)S(1)}, f32[96,96]{1,0:T(8,128)}, u32[]{:S(2)}) copy-start(f32[96,96]{1,0:T(8,128)} %constant.46.clone.y_back) | copy-start | bytes 110596
